TPU v7x, 128 devices: a whole 4x4x4 slice. The times are simulated.
128 devices in a mesh: ty: 8 (over x, core), tx: 16 (over z, y).
Axes of the slice: x: 4, y: 4, z: 4, core: 2. Of those that a mesh axis runs over, the one named last changes fastest.
Arguments:
- velocity: float32 [2, 3, 1024, 2048], P(None, None, 'ty', 'tx'), may hold values from -6 to 6
- start_position: float32 [2, 65536], P(None, ('ty', 'tx')), may hold values from 0 to 128, as said below
- cells: int32 [2, 4, 2, 65536], P(None, None, None, ('ty', 'tx')), may hold values from -1 to 127, as said below
- history: float32 [2, 71, 65536], P(None, None, ('ty', 'tx')), may hold values from -6 to 6
- leavers: int32 [1, 8], replicated, may hold values from 1 to 16, as said below
- owner: int32 [65536, 1], P(('ty', 'tx')), may hold values from 0 to 127; in each aligned block of 512 rows (0 to 511, 512 to 1023, ...) at most 16 rows name the same one
- filter_matrix: float32 [73, 73], replicated, may hold values from -0.75 to 0.75
Outputs:
- filtered: float32 [2, 73, 262144], P(None, None, ('ty', 'tx'))
Inputs may be any that keep to these rules, and one draw needn't show every extreme that they name: `start_position`: coordinates in cell units of the particle's tile. First coordinate cells lie in -1 .. 127 and second in -1 .. 127. Each move has one direction with exactly 16 leavers. Among the 512 slots of one tile no owner appears more than 16 times.
All inputs are finite; a program needn't handle non-finite values.
Results may differ from a plain program's by a relative error of at most 0.0003.
Values sent between devices are 32-bit elements; how exact they have to be, the bound alone decides.
A program may use at most 64 MiB of HBM per device.

v0:
```python
import jax
import jax.numpy as jnp
from jax import lax
from jax.sharding import PartitionSpec as P

STEPS = 2
SAMPLES = 73
HISTORY = 71
MOST = 16


drift = 0.2
moves = ((-1, -1), (-1, 0), (-1, 1), (0, -1), (0, 1), (1, -1), (1, 0), (1, 1))


def shifted(value, axis, by):
    peers = lax.axis_size(axis)
    return lax.ppermute(value, axis, [(i, (i + by) % peers) for i in range(peers)])


def padded_2(block, sides, width):
    for axis, dim in sides:
        count = lax.axis_size(axis)
        forward = [(i, i + 1) for i in range(count - 1)]
        forward.append((count - 1, 0))
        backward = [(target, source) for source, target in forward]
        low = lax.ppermute(
            lax.slice_in_dim(block, block.shape[dim] - width, None, axis=dim), axis, forward
        )
        high = lax.ppermute(lax.slice_in_dim(block, 0, width, axis=dim), axis, backward)
        block = jnp.concatenate([low, block, high], axis=dim)
    return block


def stacked_corners(plane, width):
    extent = plane.shape[1]
    widened = jnp.pad(plane, ((0, 0), (0, width + 1)))
    pieces = [widened[:, offset : offset + extent] for offset in (0, 1, width, width + 1)]
    return jnp.concatenate(pieces, axis=0)


def bilinear(corner_table, point, cell, width):
    corner = (cell[0] + 1) * width + cell[1] + 1
    wy = point[0] - cell[0].astype(jnp.float32)
    wx = point[1] - cell[1].astype(jnp.float32)
    gathered = jnp.take(corner_table, corner, axis=1)
    first = gathered[0:2]
    second = gathered[2:4]
    third = gathered[4:6]
    fourth = gathered[6:8]
    return (1.0 - wy) * ((1.0 - wx) * first + wx * second) + wy * ((1.0 - wx) * third + wx * fourth)


def apply_filter(filter_matrix, columns):
    shaped = columns.reshape(2, SAMPLES, -1)
    return jnp.einsum("tj,cjn->ctn", filter_matrix, shaped, precision=lax.Precision.HIGHEST)


def migrate(record, counts, step, tile_rows, tile_cols):
    band = step * 8 * MOST
    offsets = jnp.cumsum(counts) - counts
    starts = [band + offsets[j] for j in range(8)]
    blocks = [lax.dynamic_slice_in_dim(record, starts[j], MOST, 1) for j in range(8)]
    after_cols = list(blocks)
    for sign, members in ((1, (2, 4, 7)), (-1, (0, 3, 5))):
        stacked = jnp.stack([blocks[j] for j in members])
        arrived = shifted(stacked, "tx", sign)
        for number, j in enumerate(members):
            after_cols[j] = arrived[number]
    moved = list(after_cols)
    for sign, members in ((-1, (0, 1, 2)), (1, (5, 6, 7))):
        stacked = jnp.stack([after_cols[j] for j in members])
        arrived = shifted(stacked, "ty", sign)
        for number, j in enumerate(members):
            moved[j] = arrived[number]
    keep = lax.broadcasted_iota(jnp.int32, (1, MOST), 1)
    for j in range(8):
        dy, dx = moves[j]
        piece = moved[j].at[0].add(-dy * tile_rows).at[1].add(-dx * tile_cols)
        current = lax.dynamic_slice_in_dim(record, starts[j], MOST, 1)
        merged = jnp.where(keep < counts[j], piece, current)
        record = lax.dynamic_update_slice_in_dim(record, merged, starts[j], 1)
    return record


def per_device(velocity, start_position, cells, history, leavers, owner, filter_matrix):
    tile_rows = velocity.shape[2]
    tile_cols = velocity.shape[3]
    slots = start_position.shape[1]
    padded = padded_2(velocity, (("ty", 2), ("tx", 3)), 1)
    width = tile_cols + 2
    planes = [padded[:, a].reshape(2, (tile_rows + 2) * width) for a in range(STEPS + 1)]
    snapshot_tables = [stacked_corners(plane, width) for plane in planes]
    halfway_tables = [
        stacked_corners(0.5 * (planes[a] + planes[a + 1]), width) for a in range(STEPS)
    ]
    series = jnp.concatenate([history, jnp.zeros((2, STEPS, slots), jnp.float32)], axis=1)
    record = jnp.concatenate([start_position, series.reshape(2 * SAMPLES, slots)], axis=0)
    for step in range(STEPS):
        point = record[0:2]
        section_cells = cells[step]
        k_one = bilinear(snapshot_tables[step], point, section_cells[0], width)
        spot = point + 0.5 * drift * k_one
        k_two = bilinear(halfway_tables[step], spot, section_cells[1], width)
        spot = point + 0.5 * drift * k_two
        k_three = bilinear(halfway_tables[step], spot, section_cells[2], width)
        spot = point + drift * k_three
        k_four = bilinear(snapshot_tables[step + 1], spot, section_cells[3], width)
        point = point + drift / 6.0 * (k_one + 2.0 * k_two + 2.0 * k_three + k_four)
        record = record.at[0:2].set(point)
        record = record.at[2 + HISTORY + step].set(k_one[0])
        record = record.at[2 + SAMPLES + HISTORY + step].set(k_one[1])
        if step < STEPS - 1:
            record = migrate(record, leavers[step], step, float(tile_rows), float(tile_cols))
    columns = record[2:]
    tile_count = lax.axis_size("ty") * lax.axis_size("tx")
    per_owner = 4 * slots // tile_count
    owned = owner[:, 0]
    labels = jnp.arange(tile_count, dtype=jnp.int32)[:, None]
    onehot = (owned[None, :] == labels).astype(jnp.int32)
    running = jnp.cumsum(onehot, axis=1)
    ranks = jnp.sum(running * onehot, axis=0) - 1
    target = owned * per_owner + ranks
    outgoing = (
        jnp.zeros((2 * SAMPLES, tile_count * per_owner), jnp.float32).at[:, target].set(columns)
    )
    arrived = lax.all_to_all(outgoing, ("ty", "tx"), split_axis=1, concat_axis=1, tiled=True)
    return apply_filter(filter_matrix, arrived)


def solution(mesh):
    placed = (
        P(None, None, "ty", "tx"),
        P(None, ("ty", "tx")),
        P(None, None, None, ("ty", "tx")),
        P(None, None, ("ty", "tx")),
        P(),
        P(("ty", "tx"), None),
        P(),
    )
    return jax.shard_map(
        per_device,
        mesh=mesh,
        in_specs=placed,
        out_specs=P(None, None, ("ty", "tx")),
        check_vma=False,
    )
```

profile of v0, /device:TPU:1, one launch (start us, length us, event | category | flops | bytes accessed | tf_op | source)
XLA Modules:
  0.0 176.1 jit_solution(9661614375069935504)
XLA Ops:
  0.0 0.8 fusion.63
  0.8 2.6 %collective-permute-start = (f32[2,3,1,128]{3,2,1,0:T(1,128)S(1)}, f32[2,3,1,128]{3,2,1,0:T(1,128)S(1)}, u32[]{:S(2)}, u32[]{:S(2)}) collective-permute-start(f32[2,3,1,128]{3,2,1,0:T(1,128)S(1)} %get-tuple-element.319), channel_id=1, source_target_pairs={{0,16},{16,32},{32,48},{48,64},{64,80},{80,96},{96,112},{112,0},{1... | collective-permute-start | bytes 9224 | tf_op jit(solution)/shard_map/ppermute | solution.py:27
  3.4 0.9 add_add_fusion.3
  4.4 0.8 broadcast_subtract_fusion.14
  5.3 1.0 copy.319
  6.4 0.7 pad_maximum_fusion.7
  7.1 0.7 fusion.68
  8.0 0.7 fusion.69
  9.3 0.7 iota_compare_fusion.8
  10.5 0.6 iota_compare_fusion.6
  11.1 0.6 iota_compare_fusion.5
  11.8 0.6 iota_compare_fusion.4
  12.9 2.4 %select_reduce_fusion = s32[4,128]{0,1:T(8,128)S(1)} fusion(s32[128,4,128]{0,1,2:T(4,128)S(1)} %fusion.3, s32[128,4]{0,1:T(4,128)S(1)} %slice.822, s32[4,128]{0,1:T(8,128)S(1)} %copy.283), kind=kLoop, calls=%fused_computation.22 | loop fusion | flops 261632 | bytes 268288 | tf_op jit(solution)/shard_map/reduce_sum | solution.py:122
  15.3 0.7 iota_compare_fusion.3
  16.3 1.4 collective-permute-start.2
  17.7 5.0 %collective-permute-start.3 = (f32[2,3,130,1]{3,2,1,0:T(8,128)S(1)}, f32[2,3,130,1]{3,2,1,0:T(8,128)S(1)}, u32[]{:S(2)}, u32[]{:S(2)}) collective-permute-start(f32[2,3,130,1]{3,2,1,0:T(8,128)S(1)} %get-tuple-element.318), channel_id=1, source_target_pairs={{1,0},{2,1},{3,2},{4,3},{5,4},{6,5},{7,6},{8,7},{9,8},{10,9},{11,1... | collective-permute-start | bytes 9368 | tf_op jit(solution)/shard_map/ppermute | solution.py:30
  22.7 0.6 iota_compare_fusion.2
  39.3 1.4 add_multiply_fusion
  41.7 5.4 %copy.286 = f32[8,16900]{0,1:T(8,128)} copy(f32[8,16900]{1,0:T(8,128)S(1)} %get-tuple-element.424) | data formatting | bytes 1081600 | tf_op jit(solution)/shard_map/concatenate | solution.py:39
  47.1 4.5 %gather_fusion = f32[512,8]{1,0:T(8,128)S(1)} fusion(f32[8,16900]{0,1:T(8,128)} %copy.286, s32[1024]{0:T(1024)S(1)} %pad_clamp_fusion.7), kind=kCustom, calls=%fused_computation.clone | custom fusion | bytes 34816 | tf_op jit(solution)/shard_map/jit(_take)/gather | solution.py:46
  51.7 5.4 %copy.288 = f32[8,16900]{0,1:T(8,128)} copy(f32[8,16900]{1,0:T(8,128)S(1)} %get-tuple-element.425) | data formatting | bytes 1081600 | tf_op jit(solution)/shard_map/concatenate | solution.py:39
  57.1 4.5 %gather_fusion.1 = f32[512,8]{1,0:T(8,128)S(1)} fusion(f32[8,16900]{0,1:T(8,128)} %copy.288, s32[1024]{0:T(1024)S(1)} %pad_clamp_fusion.6), kind=kCustom, calls=%fused_computation.1.clone | custom fusion | bytes 34816 | tf_op jit(solution)/shard_map/jit(_take)/gather | solution.py:46
  61.8 4.5 %gather_fusion.2 = f32[512,8]{1,0:T(8,128)S(1)} fusion(f32[8,16900]{0,1:T(8,128)} %copy.288, s32[1024]{0:T(1024)S(1)} %pad_clamp_fusion.5), kind=kCustom, calls=%fused_computation.2.clone | custom fusion | bytes 34816 | tf_op jit(solution)/shard_map/jit(_take)/gather | solution.py:46
  67.4 5.4 %copy.292 = f32[8,16900]{0,1:T(8,128)} copy(f32[8,16900]{1,0:T(8,128)S(1)} %get-tuple-element.426) | data formatting | bytes 1081600 | tf_op jit(solution)/shard_map/concatenate | solution.py:39
  72.8 4.5 %gather_fusion.3 = f32[512,8]{1,0:T(8,128)S(1)} fusion(f32[8,16900]{0,1:T(8,128)} %copy.292, s32[1024]{0:T(1024)S(1)} %pad_clamp_fusion.4), kind=kCustom, calls=%fused_computation.3.clone | custom fusion | bytes 34816 | tf_op jit(solution)/shard_map/jit(_take)/gather | solution.py:46
  78.2 1.6 collective-permute-start.4
  80.3 4.5 %gather_fusion.4 = f32[512,8]{1,0:T(8,128)S(1)} fusion(f32[8,16900]{0,1:T(8,128)} %copy.292, s32[1024]{0:T(1024)S(1)} %pad_clamp_fusion.3), kind=kCustom, calls=%fused_computation.4.clone | custom fusion | bytes 34816 | tf_op jit(solution)/shard_map/jit(_take)/gather | solution.py:46
  84.9 5.4 %copy.308 = f32[8,16900]{0,1:T(8,128)} copy(f32[8,16900]{1,0:T(8,128)S(1)} %get-tuple-element.427) | data formatting | bytes 1081600 | tf_op jit(solution)/shard_map/concatenate | solution.py:39
  90.3 4.5 %gather_fusion.5 = f32[512,8]{1,0:T(8,128)S(1)} fusion(f32[8,16900]{0,1:T(8,128)} %copy.308, s32[1024]{0:T(1024)S(1)} %pad_clamp_fusion.2), kind=kCustom, calls=%fused_computation.5.clone | custom fusion | bytes 34816 | tf_op jit(solution)/shard_map/jit(_take)/gather | solution.py:46
  94.8 4.5 %gather_fusion.6 = f32[512,8]{1,0:T(8,128)S(1)} fusion(f32[8,16900]{0,1:T(8,128)} %copy.308, s32[1024]{0:T(1024)S(1)} %pad_clamp_fusion.1), kind=kCustom, calls=%fused_computation.6.clone | custom fusion | bytes 34816 | tf_op jit(solution)/shard_map/jit(_take)/gather | solution.py:46
  99.7 5.4 %copy.312 = f32[8,16900]{0,1:T(8,128)} copy(f32[8,16900]{1,0:T(8,128)S(1)} %pad_maximum_fusion.5) | data formatting | bytes 1081600 | tf_op jit(solution)/shard_map/concatenate | solution.py:39
  105.1 4.5 %gather_fusion.7 = f32[512,8]{1,0:T(8,128)S(1)} fusion(f32[8,16900]{0,1:T(8,128)} %copy.312, s32[1024]{0:T(1024)S(1)} %pad_clamp_fusion), kind=kCustom, calls=%fused_computation.7.clone | custom fusion | bytes 34816 | tf_op jit(solution)/shard_map/jit(_take)/gather | solution.py:46
  109.8 2.6 %collective-permute-start.7 = (f32[3,148,16]{2,1,0:T(8,128)S(1)}, f32[3,148,16]{2,1,0:T(8,128)S(1)}, u32[]{:S(2)}, u32[]{:S(2)}) collective-permute-start(f32[3,148,16]{2,1,0:T(8,128)S(1)} %pad_maximum_fusion.9), channel_id=1, source_target_pairs={{0,16},{16,32},{32,48},{48,64},{64,80},{80,96},{96,112},{112,0},{1... | collective-permute-start | bytes 85256 | tf_op jit(solution)/shard_map/ppermute | solution.py:18
  112.8 2.6 %collective-permute-done.7 = f32[3,148,16]{2,1,0:T(8,128)S(1)} collective-permute-done((f32[3,148,16]{2,1,0:T(8,128)S(1)}, f32[3,148,16]{2,1,0:T(8,128)S(1)}, u32[]{:S(2)}, u32[]{:S(2)}) %collective-permute-start.7) | collective-permute-done | bytes 28448 | tf_op jit(solution)/shard_map/ppermute | solution.py:18
  115.7 2.7 %collective-permute-done.6 = f32[3,148,16]{2,1,0:T(8,128)S(1)} collective-permute-done((f32[3,148,16]{2,1,0:T(8,128)S(1)}, f32[3,148,16]{2,1,0:T(8,128)S(1)}, u32[]{:S(2)}, u32[]{:S(2)}) %collective-permute-start.6) | collective-permute-done | bytes 28448 | tf_op jit(solution)/shard_map/ppermute | solution.py:18
  118.7 0.8 dynamic_update_slice.24
  119.6 1.0 dynamic_update_slice.25
  120.6 1.0 dynamic_update_slice.26
  121.7 1.0 dynamic_update_slice.27
  122.8 1.0 dynamic_update_slice.28
  123.9 1.0 dynamic_update_slice.29
  124.9 1.0 dynamic_update_slice.30
  126.0 1.0 dynamic_update_slice.31
  127.6 2.8 %scatter_custom_fusion = f32[146,2048]{0,1:T(8,128)S(1)} fusion(s32[512]{0:T(512)S(1)} %bitcast.240, f32[512,146]{1,0:T(8,128)S(1)} %copy.314, f32[]{:T(128)} %constant.530.clone.1), kind=kCustom, calls=%fused_computation.11 | custom fusion | bytes 1196036 | tf_op jit(solution)/shard_map/scatter | solution.py:125
  130.3 38.7 %all_to_all.9 = f32[146,128,16]{0,2,1:T(8,128)} all-to-all(f32[146,128,16]{0,2,1:T(8,128)S(1)} %bitcast.182), channel_id=1, replica_groups=mesh['ty'=8,'tx'=16] {'ty','tx'}, dimensions={1} | all-to-all | bytes 2392064 | tf_op jit(solution)/shard_map/all_to_all | solution.py:127
  169.1 2.6 %reshape.952 = f32[2,73,2048]{1,0,2:T(2,128)S(1)} reshape(f32[146,128,16]{0,2,1:T(8,128)} %all_to_all.9) | data formatting | bytes 2392064 | tf_op jit(solution)/shard_map/reshape | solution.py:55
  171.7 2.5 %convolution_bitcast_fusion = f32[2,73,2048]{2,1,0:T(8,128)S(1)} fusion(f32[2,73,2048]{1,0,2:T(2,128)S(1)} %reshape.952, f32[73,73]{1,0:T(8,128)S(1)} %copy-done), kind=kOutput, calls=%fused_computation.9 | convolution fusion | flops 261931008 | bytes 2413380 | tf_op jit(solution)/shard_map/tj,cjn->ctn/dot_general | solution.py:56
  174.2 1.9 %copy.316 = f32[2,73,2048]{2,0,1:T(2,128)} copy(f32[2,73,2048]{2,1,0:T(8,128)S(1)} %convolution_bitcast_fusion) | data formatting | bytes 2392064 | tf_op jit(solution)/shard_map/tj,cjn->ctn/transpose | solution.py:56
  (155 shorter events, 10.1 us)
Async XLA Ops:
  0.0 171.7 %copy-start = (f32[73,73]{1,0:T(8,128)S(1)}, f32[73,73]{1,0:T(8,128)}, u32[]{:S(2)}) copy-start(f32[73,73]{1,0:T(8,128)} %param.59) | copy-start | bytes 63952
  0.0 16.1 %copy-start.1 = (f32[2,3,128,128]{3,2,1,0:T(8,128)S(1)}, f32[2,3,128,128]{3,2,1,0:T(8,128)}, u32[]{:S(2)}) copy-start(f32[2,3,128,128]{3,2,1,0:T(8,128)} %param.53) | copy-start | bytes 1179652
  0.0 7.1 %copy-start.4 = (s32[1,8]{1,0:T(1,128)S(1)}, s32[1,8]{1,0:T(1,128)}, u32[]{:S(2)}) copy-start(s32[1,8]{1,0:T(1,128)} %param.57) | copy-start | bytes 100
  0.0 12.5 %copy-start.5 = (s32[512,1]{0,1:T(1,128)S(1)}, s32[512,1]{0,1:T(1,128)}, u32[]{:S(2)}) copy-start(s32[512,1]{0,1:T(1,128)} %param.58) | copy-start | bytes 6148
  0.8 15.2 %collective-permute-start = (f32[2,3,1,128]{3,2,1,0:T(1,128)S(1)}, f32[2,3,1,128]{3,2,1,0:T(1,128)S(1)}, u32[]{:S(2)}, u32[]{:S(2)}) collective-permute-start(f32[2,3,1,128]{3,2,1,0:T(1,128)S(1)} %get-tuple-element.319), channel_id=1, source_target_pairs={{0,16},{16,32},{32,48},{48,64},{64,80},{80,96},{96,112},{112,0},{1... | collective-permute-start | bytes 9224 | tf_op jit(solution)/shard_map/ppermute | solution.py:27
  3.4 12.6 %collective-permute-start.1 = (f32[2,3,1,128]{3,2,1,0:T(1,128)S(1)}, f32[2,3,1,128]{3,2,1,0:T(1,128)S(1)}, u32[]{:S(2)}, u32[]{:S(2)}) collective-permute-start(f32[2,3,1,128]{3,2,1,0:T(1,128)S(1)} %get-tuple-element.320), channel_id=1, source_target_pairs={{16,0},{32,16},{48,32},{64,48},{80,64},{96,80},{112,96},{0,112},{1... | collective-permute-start | bytes 9224 | tf_op jit(solution)/shard_map/ppermute | solution.py:30
  16.3 21.6 %collective-permute-start.2 = (f32[2,3,130,1]{3,2,1,0:T(8,128)S(1)}, f32[2,3,130,1]{3,2,1,0:T(8,128)S(1)}, u32[]{:S(2)}, u32[]{:S(2)}) collective-permute-start(f32[2,3,130,1]{3,2,1,0:T(8,128)S(1)} %get-tuple-element.317), channel_id=1, source_target_pairs={{0,1},{1,2},{2,3},{3,4},{4,5},{5,6},{6,7},{7,8},{8,9},{9,10},{10,1... | collective-permute-start | bytes 9368 | tf_op jit(solution)/shard_map/ppermute | solution.py:27
  17.7 20.3 %collective-permute-start.3 = (f32[2,3,130,1]{3,2,1,0:T(8,128)S(1)}, f32[2,3,130,1]{3,2,1,0:T(8,128)S(1)}, u32[]{:S(2)}, u32[]{:S(2)}) collective-permute-start(f32[2,3,130,1]{3,2,1,0:T(8,128)S(1)} %get-tuple-element.318), channel_id=1, source_target_pairs={{1,0},{2,1},{3,2},{4,3},{5,4},{6,5},{7,6},{8,7},{9,8},{10,9},{11,1... | collective-permute-start | bytes 9368 | tf_op jit(solution)/shard_map/ppermute | solution.py:30
  41.7 10.0 %copy-start.2 = (f32[2,512]{1,0:T(2,128)S(1)}, f32[2,512]{1,0:T(2,128)}, u32[]{:S(2)}) copy-start(f32[2,512]{1,0:T(2,128)} %param.54) | copy-start | bytes 12292
  41.7 10.0 %copy-start.3 = (s32[2,4,2,512]{3,2,1,0:T(2,128)S(1)}, s32[2,4,2,512]{3,2,1,0:T(2,128)}, u32[]{:S(2)}) copy-start(s32[2,4,2,512]{3,2,1,0:T(2,128)} %param.55) | copy-start | bytes 98308
  78.2 31.5 %collective-permute-start.4 = (f32[3,148,16]{2,1,0:T(8,128)S(1)}, f32[3,148,16]{2,1,0:T(8,128)S(1)}, u32[]{:S(2)}, u32[]{:S(2)}) collective-permute-start(f32[3,148,16]{2,1,0:T(8,128)S(1)} %copy.297), channel_id=1, source_target_pairs={{0,15},{1,0},{2,1},{3,2},{4,3},{5,4},{6,5},{7,6},{8,7},{9,8},{10,9... | collective-permute-start | bytes 85256 | tf_op jit(solution)/shard_map/ppermute | solution.py:18
  80.2 29.6 %collective-permute-start.5 = (f32[3,148,16]{2,1,0:T(8,128)S(1)}, f32[3,148,16]{2,1,0:T(8,128)S(1)}, u32[]{:S(2)}, u32[]{:S(2)}) collective-permute-start(f32[3,148,16]{2,1,0:T(8,128)S(1)} %copy.302), channel_id=1, source_target_pairs={{0,1},{1,2},{2,3},{3,4},{4,5},{5,6},{6,7},{7,8},{8,9},{9,10},{10,1... | collective-permute-start | bytes 85256 | tf_op jit(solution)/shard_map/ppermute | solution.py:18
  109.8 5.6 %collective-permute-start.7 = (f32[3,148,16]{2,1,0:T(8,128)S(1)}, f32[3,148,16]{2,1,0:T(8,128)S(1)}, u32[]{:S(2)}, u32[]{:S(2)}) collective-permute-start(f32[3,148,16]{2,1,0:T(8,128)S(1)} %pad_maximum_fusion.9), channel_id=1, source_target_pairs={{0,16},{16,32},{32,48},{48,64},{64,80},{80,96},{96,112},{112,0},{1... | collective-permute-start | bytes 85256 | tf_op jit(solution)/shard_map/ppermute | solution.py:18
  112.6 5.8 %collective-permute-start.6 = (f32[3,148,16]{2,1,0:T(8,128)S(1)}, f32[3,148,16]{2,1,0:T(8,128)S(1)}, u32[]{:S(2)}, u32[]{:S(2)}) collective-permute-start(f32[3,148,16]{2,1,0:T(8,128)S(1)} %pad_maximum_fusion.8), channel_id=1, source_target_pairs={{0,112},{16,0},{32,16},{48,32},{64,48},{80,64},{96,80},{112,96},{1... | collective-permute-start | bytes 85256 | tf_op jit(solution)/shard_map/ppermute | solution.py:18
where the time goes:
time: 177 us; the launch traced here: 176 us
  local copies, waits for them, and re-layouts  85.9 us (49%)
  blocking collectives  38.7 us (22%)
  between operations  15.5 us (9%)
  other arithmetic  14.6 us (8%)
  starting transfers between devices  13.5 us (8%)
  waiting for transfers between devices  5.35 us (3%)
  matrix products  2.46 us (1%)
    all_to_all x1, blocking collectives, per_device(): lax.all_to_all(outgoing, ('ty', 'tx'), split_axis=1, concat_axis=1, tiled...  38.7 us
    gather x16, local copies, waits for them, and re-layouts, bilinear(): gathered = jnp.take(corner_table, corner, axis=1)  36.6 us
    concatenate x5, local copies, waits for them, and re-layouts, stacked_corners(): return jnp.concatenate(pieces, axis=0)  26.8 us
    dynamic_update_slice x8, local copies, waits for them, and re-layouts, migrate(): record = lax.dynamic_update_slice_in_dim(record, merged, starts[j], 1)  7.5 us
    ppermute x4, waiting for transfers between devices, shifted(): lax.ppermute(value, axis, [(i, (i + by) % peers) for i in range(peers)])  5.34 us
    lt x8, other arithmetic, migrate(): merged = jnp.where(keep < counts[j], piece, current)  5.05 us
    ppermute x2, starting transfers between devices, padded_2(): lax.ppermute(lax.slice_in_dim(block, 0, width, axis=dim), axis, backward)  5 us
    ppermute x4, starting transfers between devices, shifted(): lax.ppermute(value, axis, [(i, (i + by) % peers) for i in range(peers)])  4.54 us
  transfers between devices with their start and end apart: 8, of which 2 were waited for; matrix products, arithmetic and copies ran while one was open for 24% of the time, Pallas kernels for 0%

commit v1 on v0

v1 whole, which is shorter than its diff:
```python
import jax
import jax.numpy as jnp
from jax import lax
from jax.experimental import pallas as pl
from jax.experimental.pallas import tpu as pltpu
from jax.sharding import PartitionSpec as P

STEPS = 2
SAMPLES = 73
HISTORY = 71
MOST = 16
ROWS = 19

drift = 0.2
moves = ((-1, -1), (-1, 0), (-1, 1), (0, -1), (0, 1), (1, -1), (1, 0), (1, 1))
MESH = pl.DeviceIdType.MESH
f32 = jnp.float32
bf16 = jnp.bfloat16
i32 = jnp.int32
NT = (((1,), (1,)), ((), ()))
TN = (((0,), (0,)), ((), ()))


def iota(shape, dim):
    return lax.broadcasted_iota(i32, shape, dim)


def halves(x):
    high = x.astype(bf16)
    return high, (x - high.astype(f32)).astype(bf16)


def dot(a, b, dims=(((1,), (0,)), ((), ()))):
    return lax.dot_general(a, b, dims, preferred_element_type=f32)


def swap_blocks(x):
    sub = iota((8, 128), 0)
    block = iota((8, 128), 1) // 16
    for b in (1, 2, 4):
        row_bit = (sub // b) % 2
        col_bit = (block // b) % 2
        down = pltpu.roll(pltpu.roll(x, b, 0), 128 - 16 * b, 1)
        up = pltpu.roll(pltpu.roll(x, 8 - b, 0), 16 * b, 1)
        x = jnp.where(row_bit > col_bit, down, jnp.where(row_bit < col_bit, up, x))
    return x


def lookup(table, index):
    held = jnp.minimum(jnp.maximum(index, 0), 127)
    parts = []
    for n in range(4):
        at = jnp.broadcast_to(held[:, 128 * n : 128 * n + 128], (8, 128))
        parts.append(jnp.take_along_axis(table, at, axis=1))
    return jnp.concatenate(parts, axis=1)


def advance_kernel(
    leavers_ref, velocity_ref, start_ref, cells_ref, history_ref, owner_col_ref, owner_row_ref, filter_ref,
    arrived_ref, end_ref,
    planes, edges, edges_in, packed, packed_in, spots, spots_in, corners, split_low, message,
    edge_send, edge_recv, packed_send, packed_recv, spot_send, spot_recv, send_sem, recv_sem, own_sem,
):
    ty = lax.axis_index("ty")
    tx = lax.axis_index("tx")
    me = ty * 16 + tx
    barrier = pltpu.get_barrier_semaphore()

    def greet(k, carry):
        peer = lax.rem(me + k, 128)
        pl.semaphore_signal(barrier, inc=1, device_id=(peer // 16, lax.rem(peer, 16)), device_id_type=MESH)
        return carry

    lax.fori_loop(1, 128, greet, 0)

    def neighbour(j):
        dy, dx = moves[j]
        return (lax.rem(ty + dy + 8, 8), lax.rem(tx + dx + 16, 16))

    for a in range(3):
        for c in range(2):
            high, low = halves(velocity_ref[c, a])
            planes[2 * a, 128 * c : 128 * c + 128, 0:128] = high
            planes[2 * a, 128 * c : 128 * c + 128, 128:256] = low
    pick_row = iota((8, 256), 0)
    pick_lane = iota((8, 256), 1) % 128
    pick = ((pick_lane == 0) & (pick_row == 0)) | ((pick_lane == 127) & (pick_row == 1))
    pick = jnp.where(pick, 1.0, 0.0).astype(bf16)
    for a in range(3):
        sides = dot(pick, planes[2 * a], NT)
        for c in range(2):
            r = 3 * c + a
            edges[0, r : r + 1, :] = velocity_ref[c, a, 0:1, :]
            edges[1, r : r + 1, :] = velocity_ref[c, a, 127:128, :]
            edges[2, r : r + 1, :] = sides[0:1, 128 * c : 128 * c + 128]
            edges[3, r : r + 1, :] = sides[1:2, 128 * c : 128 * c + 128]
    for kind in range(4):
        edges[kind, 6:8, :] = jnp.zeros((2, 128), f32)

    counts = [leavers_ref[0, j] for j in range(8)]
    starts = [0]
    for j in range(8):
        starts.append(starts[j] + counts[j])
    place = iota((128, 128), 0) % 16
    way = iota((128, 128), 0) // 16
    first = jnp.zeros((128, 128), i32)
    many = jnp.zeros((128, 128), i32)
    for j in range(8):
        first = jnp.where(way == j, starts[j], first)
        many = jnp.where(way == j, counts[j], many)
    leaving = (iota((128, 128), 1) == first + place) & (place < many)
    leaving = jnp.where(leaving, 1.0, 0.0).astype(bf16)
    for c in range(2):
        high, low = halves(history_ref[c, :, 0:128])
        block = dot(leaving, high, NT) + dot(leaving, low, NT)
        packed[:, :, 128 * c : 128 * c + HISTORY] = block.reshape(8, 16, HISTORY)

    pl.semaphore_wait(barrier, 127)

    edge_copies = []
    packed_copies = []
    spot_copies = []
    for j in range(8):
        dy, dx = moves[j]
        kind = {1: 1, -1: 0}.get(dy, 3 if dx == 1 else 2)
        edge_copies.append(pltpu.make_async_remote_copy(
            src_ref=edges.at[kind], dst_ref=edges_in.at[j], send_sem=edge_send.at[j], recv_sem=edge_recv.at[j],
            device_id=neighbour(j), device_id_type=MESH))
        packed_copies.append(pltpu.make_async_remote_copy(
            src_ref=packed.at[j], dst_ref=packed_in.at[j], send_sem=packed_send.at[j], recv_sem=packed_recv.at[j],
            device_id=neighbour(j), device_id_type=MESH))
        spot_copies.append(pltpu.make_async_remote_copy(
            src_ref=spots, dst_ref=spots_in.at[j], send_sem=spot_send.at[j], recv_sem=spot_recv.at[j],
            device_id=neighbour(j), device_id_type=MESH))
    for copy in edge_copies:
        copy.start()
    for copy in packed_copies:
        copy.start()

    for a in range(2):
        for c in range(2):
            high, low = halves(0.5 * (velocity_ref[c, a] + velocity_ref[c, a + 1]))
            planes[2 * a + 1, 128 * c : 128 * c + 128, 0:128] = high
            planes[2 * a + 1, 128 * c : 128 * c + 128, 128:256] = low

    def gather(section, carry):
        plane = planes[2 * (section // 4) + (section % 4 + 1) // 2]
        cell_y = cells_ref[2 * section]
        cell_x = cells_ref[2 * section + 1]
        column = iota((256, 512), 0) % 128
        row = iota((128, 512), 0)
        for dx in range(2):
            chosen = jnp.where(column == cell_x + dx, 1.0, 0.0).astype(bf16)
            along = dot(plane, chosen)
            for dy in range(2):
                on = row == cell_y + dy
                for c in range(2):
                    part = jnp.where(on, along[128 * c : 128 * c + 128], 0.0)
                    at = 4 * dy + 2 * dx + c
                    corners[section, at : at + 1, :] = jnp.sum(part, axis=0, keepdims=True)
        return carry

    lax.fori_loop(0, 8, gather, 0)

    same = (owner_col_ref[...] == owner_row_ref[...]) & (iota((512, 512), 0) < iota((512, 512), 1))
    rank = jnp.sum(jnp.where(same, 1.0, 0.0), axis=0, keepdims=True).astype(i32)
    target = owner_row_ref[...] * 16 + rank

    for copy in edge_copies:
        copy.wait_recv()
    where_from = {move: j for j, move in enumerate(moves)}
    top = edges_in[where_from[(1, 0)]]
    bottom = edges_in[where_from[(-1, 0)]]
    left = edges_in[where_from[(0, 1)]]
    right = edges_in[where_from[(0, -1)]]
    top_left = edges_in[where_from[(1, 1)]][:, 127:128]
    top_right = edges_in[where_from[(1, -1)]][:, 0:1]
    bottom_left = edges_in[where_from[(-1, 1)]][:, 127:128]
    bottom_right = edges_in[where_from[(-1, -1)]][:, 0:1]

    def cell_of(section):
        return cells_ref[2 * section], cells_ref[2 * section + 1]

    def all_corners(section):
        step, part = section // 4, section % 4
        cell_y, cell_x = cell_of(section)
        sides = {}
        for dy in range(2):
            yy = cell_y + dy
            sides[dy] = (lookup(left, yy), lookup(right, yy))
        result = []
        ends = {}
        for dx in range(2):
            xx = cell_x + dx
            ends[dx] = tuple(
                jnp.where(xx < 0, lower, jnp.where(xx > 127, upper, lookup(line, xx)))
                for line, lower, upper in ((top, top_left, top_right), (bottom, bottom_left, bottom_right)))
        for dy in range(2):
            for dx in range(2):
                yy, xx = cell_y + dy, cell_x + dx
                outer = jnp.where(xx < 0, sides[dy][0], jnp.where(xx > 127, sides[dy][1], 0.0))
                outer = jnp.where(yy < 0, ends[dx][0], jnp.where(yy > 127, ends[dx][1], outer))
                rows = []
                for c in range(2):
                    a = step + (part == 3)
                    value = outer[3 * c + a : 3 * c + a + 1]
                    if part in (1, 2):
                        value = 0.5 * (value + outer[3 * c + a + 1 : 3 * c + a + 2])
                    rows.append(value)
                at = 4 * dy + 2 * dx
                result.append(corners[section, at : at + 2, :] + jnp.concatenate(rows, axis=0))
        return result

    def sample(section, held, point):
        cell_y, cell_x = cell_of(section)
        wy = point[0:1] - cell_y.astype(f32)
        wx = point[1:2] - cell_x.astype(f32)
        first_c, second_c, third_c, fourth_c = held
        return (1.0 - wy) * ((1.0 - wx) * first_c + wx * second_c) + wy * ((1.0 - wx) * third_c + wx * fourth_c)

    def rest_of_step(step, held, point, k_one):
        spot = point + 0.5 * drift * k_one
        k_two = sample(4 * step + 1, held[0], spot)
        spot = point + 0.5 * drift * k_two
        k_three = sample(4 * step + 2, held[1], spot)
        spot = point + drift * k_three
        k_four = sample(4 * step + 3, held[2], spot)
        return point + drift / 6.0 * (k_one + 2.0 * k_two + 2.0 * k_three + k_four)

    point = start_ref[...]
    k_first = sample(0, all_corners(0), point)
    point = rest_of_step(0, [all_corners(s) for s in (1, 2, 3)], point, k_first)

    spots[0:2, :] = point[:, 0:128]
    spots[2:4, :] = k_first[:, 0:128]
    spots[4:8, :] = jnp.zeros((4, 128), f32)
    for copy in spot_copies:
        copy.start()

    next_corners = all_corners(4)

    for copy in packed_copies:
        copy.wait_recv()
    lane = iota((1, 128), 1)
    matrix = filter_ref[...]
    partial = []
    for c in range(2):
        block = packed_in[:, :, 128 * c : 128 * c + HISTORY].reshape(128, HISTORY)
        high, low = halves(block)
        came = dot(high, leaving, TN) + dot(low, leaving, TN)
        own = jnp.where(lane < starts[8], came, history_ref[c, :, 0:128])
        series = jnp.concatenate([own, history_ref[c, :, 128:512]], axis=1)
        partial.append(lax.dot_general(
            matrix[:, 0:HISTORY], series, (((1,), (0,)), ((), ())),
            precision=lax.Precision.HIGHEST, preferred_element_type=f32))

    for copy in spot_copies:
        copy.wait_recv()
    moved_point = point[:, 0:128]
    moved_first = k_first[:, 0:128]
    for j in range(8):
        dy, dx = moves[j]
        here = (lane >= starts[j]) & (lane < starts[j + 1])
        arrival = spots_in[j]
        shift = jnp.where(iota((2, 128), 0) == 0, float(dy * 128), float(dx * 128))
        moved_point = jnp.where(here, arrival[0:2] - shift, moved_point)
        moved_first = jnp.where(here, arrival[2:4], moved_first)
    point = jnp.concatenate([moved_point, point[:, 128:512]], axis=1)
    k_first = jnp.concatenate([moved_first, k_first[:, 128:512]], axis=1)
    k_second = sample(4, next_corners, point)

    low = [
        partial[c] + matrix[:, 71:72] * k_first[c : c + 1] + matrix[:, 72:73] * k_second[c : c + 1]
        for c in range(2)
    ]
    sub = iota((16, 512), 0)
    tail = jnp.where(sub == 0, low[0][72:73], jnp.where(sub == 1, low[1][72:73], 0.0))
    for number, at, piece in (
        (0, 0, low[0][0:64]), (1, 64, low[1][0:64]),
        (2, 128, jnp.concatenate([low[0][64:72], low[1][64:72]], axis=0)), (3, 144, tail),
    ):
        high, rest = halves(piece)
        split_low[at : at + piece.shape[0], :] = high
        split_low[160 + at : 160 + at + piece.shape[0], :] = rest

    def deliver(k, carry):
        goal = lax.rem(ty + k, 8)
        chosen = jnp.where(iota((256, 512), 0) + goal * 256 == target, 1.0, 0.0).astype(bf16)
        columns = dot(split_low[...], chosen, NT)
        columns = columns[0:160] + columns[160:320]
        for h in range(2):
            owners = pl.ds(goal * 16 + 8 * h, 8)
            wide = columns[:, 128 * h : 128 * h + 128]
            message[owners, 0:16, :] = jnp.transpose(wide[0:128]).reshape(8, 16, 128)
            for a in range(3):
                message[owners, 16 + a, :] = swap_blocks(wide[128 + 8 * a : 136 + 8 * a])

        def send(m, inner):
            column = lax.rem(tx + m, 16)
            pltpu.make_async_remote_copy(
                src_ref=message.at[goal * 16 + column, pl.ds(0, ROWS)], dst_ref=arrived_ref.at[me, pl.ds(0, ROWS)],
                send_sem=send_sem, recv_sem=recv_sem, device_id=(goal, column), device_id_type=MESH).start()
            return inner

        lax.fori_loop(1 - jnp.minimum(k, 1), 16, send, 0)
        return carry

    lax.fori_loop(0, 8, deliver, 0)
    own_copy = pltpu.make_async_copy(message.at[me, pl.ds(0, ROWS)], arrived_ref.at[me, pl.ds(0, ROWS)], own_sem)
    own_copy.start()

    end_ref[...] = rest_of_step(1, [all_corners(s) for s in (5, 6, 7)], point, k_second)

    for copy in edge_copies + packed_copies + spot_copies:
        copy.wait_send()
    own_copy.wait()
    sent = message.at[pl.ds(0, 127), pl.ds(0, ROWS)]
    pltpu.make_async_copy(sent, sent, send_sem).wait()
    landed = arrived_ref.at[pl.ds(0, 127), pl.ds(0, ROWS)]
    pltpu.make_async_copy(landed, landed, recv_sem).wait()


def spread_kernel(arrived_ref, out_ref):
    wide = jnp.transpose(arrived_ref[:, 0:16, :].reshape(256, 128))
    out_ref[0, 0:64, :] = wide[0:64]
    out_ref[1, 0:64, :] = wide[64:128]
    for h in range(2):
        lanes = pl.ds(128 * h, 128)
        for a in range(3):
            part = swap_blocks(arrived_ref[8 * h : 8 * h + 8, 16 + a, :])
            if a < 2:
                out_ref[a, 64:72, lanes] = part
            else:
                out_ref[0, 72:73, lanes] = part[0:1]
                out_ref[1, 72:73, lanes] = part[1:2]


def per_device(velocity, start_position, cells, history, leavers, owner, filter_matrix):
    vmem = pl.BlockSpec(memory_space=pltpu.VMEM)
    arrived, end = pl.pallas_call(
        advance_kernel,
        out_shape=(jax.ShapeDtypeStruct((128, 24, 128), f32), jax.ShapeDtypeStruct((2, 512), f32)),
        in_specs=[pl.BlockSpec(memory_space=pltpu.SMEM)] + [vmem] * 7,
        out_specs=(pl.BlockSpec(memory_space=pl.ANY), vmem),
        scratch_shapes=[
            pltpu.VMEM((5, 256, 256), bf16),
            pltpu.VMEM((4, 8, 128), f32),
            pltpu.VMEM((8, 8, 128), f32),
            pltpu.VMEM((8, 16, 256), f32),
            pltpu.VMEM((8, 16, 256), f32),
            pltpu.VMEM((8, 128), f32),
            pltpu.VMEM((8, 8, 128), f32),
            pltpu.VMEM((8, 8, 512), f32),
            pltpu.VMEM((320, 512), bf16),
            pltpu.VMEM((128, 24, 128), f32),
        ]
        + [pltpu.SemaphoreType.DMA((8,))] * 6
        + [pltpu.SemaphoreType.DMA] * 3,
        compiler_params=pltpu.CompilerParams(collective_id=0, has_side_effects=True),
        name="advance",
    )(
        leavers, velocity, start_position, cells.reshape(16, 1, 512), history, owner,
        owner.reshape(1, 512), filter_matrix,
    )
    return pl.pallas_call(
        spread_kernel,
        grid=(8,),
        out_shape=jax.ShapeDtypeStruct((2, SAMPLES, 2048), f32),
        in_specs=[pl.BlockSpec((16, 24, 128), lambda i: (i, 0, 0))],
        out_specs=pl.BlockSpec((2, SAMPLES, 256), lambda i: (0, 0, i)),
        name="spread",
    )(arrived)


def solution(mesh):
    placed = (
        P(None, None, "ty", "tx"),
        P(None, ("ty", "tx")),
        P(None, None, None, ("ty", "tx")),
        P(None, None, ("ty", "tx")),
        P(),
        P(("ty", "tx"), None),
        P(),
    )
    return jax.shard_map(
        per_device,
        mesh=mesh,
        in_specs=placed,
        out_specs=P(None, None, ("ty", "tx")),
        check_vma=False,
    )
```

time: 177 us -> 56.6 us (0.32)
  local copies, waits for them, and re-layouts: 85.9 us -> 7.94 us
  Pallas kernels: 0 us -> 48.2 us
  blocking collectives: 38.7 us -> 0 us
  between operations: 15.5 us -> 0.01 us
  other arithmetic: 14.6 us -> 0 us
  starting transfers between devices: 13.5 us -> 0 us
  waiting for transfers between devices: 5.35 us -> 0 us
  matrix products: 2.46 us -> 0 us
    pallas_call x0 -> x2, Pallas kernels: none -> 48.2 us  [the longest x1 41.7 us: per_device(): pl.pallas_call(advance_kernel, out_shape=(jax.ShapeDtypeStruct((128, 24,...]
    all_to_all x1 -> x0, blocking collectives: 38.7 us -> none  [per_device(): lax.all_to_all(outgoing, ('ty', 'tx'), split_axis=1, concat_axis=1, tiled...]
    gather x16 -> x0, local copies, waits for them, and re-layouts: 36.6 us -> none  [bilinear(): gathered = jnp.take(corner_table, corner, axis=1)]
    concatenate x6 -> x0, local copies, waits for them, and re-layouts: 26.9 us -> none  [the longest x5 26.8 us: stacked_corners(): return jnp.concatenate(pieces, axis=0)]
    ppermute x8 -> x0, starting transfers between devices: 13.5 us -> none  [the longest x2 5 us: padded_2(): lax.ppermute(lax.slice_in_dim(block, 0, width, axis=dim), axis, backward)]
    dynamic_update_slice x8 -> x0, local copies, waits for them, and re-layouts: 7.5 us -> none  [migrate(): record = lax.dynamic_update_slice_in_dim(record, merged, starts[j], 1)]
    ppermute x8 -> x0, waiting for transfers between devices: 5.35 us -> none  [the longest x4 5.34 us: shifted(): lax.ppermute(value, axis, [(i, (i + by) % peers) for i in range(peers)])]
    lt x8 -> x0, other arithmetic: 5.05 us -> none  [migrate(): merged = jnp.where(keep < counts[j], piece, current)]
  transfers between devices with their start and end apart: 8 -> 0, of which waited for: 2 -> 0; matrix products, arithmetic and copies ran while one was open for 24% -> 0% of each run, Pallas kernels for 0% -> 0%
where the time goes in v1:
time: 56.6 us; the launch traced here: 56.2 us
  Pallas kernels  48.2 us (85%)
  local copies, waits for them, and re-layouts  7.94 us (14%)
    pallas_call x1, Pallas kernels, per_device(): pl.pallas_call(advance_kernel, out_shape=(jax.ShapeDtypeStruct((128, 24,...  41.7 us
    pallas_call x1, Pallas kernels, per_device(): pl.pallas_call(spread_kernel, grid=(8,), out_shape=jax.ShapeDtypeStruct((...  6.48 us
    unnamed x2, local copies, waits for them, and re-layouts  3.27 us
    pallas_call x1, local copies, waits for them, and re-layouts, per_device(): pl.pallas_call(spread_kernel, grid=(8,), out_shape=jax.ShapeDtypeStruct((...  3.26 us
    reshape x1, local copies, waits for them, and re-layouts, per_device(): cells.reshape(16, 1, 512)  1.42 us

profile of v1, /device:TPU:1, one launch (start us, length us, event | category | flops | bytes accessed | tf_op | source)
XLA Modules:
  0.0 56.2 jit_solution(2572629592122493688)
XLA Ops:
  0.0 1.4 %reshape.6.cells_ref = s32[16,1,512]{2,1,0:T(1,128)} reshape(s32[2,4,2,512]{3,2,1,0:T(2,128)} %param.9) | data formatting | bytes 65536 | tf_op jit(solution)/shard_map/reshape | solution.py:362
  1.4 1.5 %copy.9.owner_col_ref = s32[512,1]{1,0:T(8,128)} copy(s32[512,1]{0,1:T(1,128)} %param.12) | data formatting | bytes 4096 | tf_op args[5]
  3.0 1.7 %copy.8.history_ref = f32[2,71,512]{2,1,0:T(8,128)} copy(f32[2,71,512]{2,0,1:T(2,128)} %param.10) | data formatting | bytes 581632 | tf_op args[3]
  4.7 41.7 %advance.1 = (f32[128,24,128]{2,1,0:T(8,128)}, f32[2,512]{1,0:T(2,128)}) custom-call(s32[1,8]{1,0:T(1,128)} %leavers_ref.1, f32[2,3,128,128]{3,2,1,0:T(8,128)} %velocity_ref.1, f32[2,512]{1,0:T(2,128)} %start_ref.1, s32[16,1,512]{2,1,0:T(1,128)} %reshape.6.cells_ref, f32[2,71,512]{2,1,0:T(8,128)} %copy.8.history_ref, s32[512,1]{1,0:T(8,128)} %copy.9.owner_col_ref, ...), custom_call_target="tpu_custom_call" | custom-call | tf_op jit(solution)/shard_map/advance/pallas_call | solution.py:340
  46.4 6.5 %spread.1 = f32[2,73,2048]{2,1,0:T(8,128)} custom-call(f32[128,24,128]{2,1,0:T(8,128)} %get-tuple-element.6.arrived_ref), custom_call_target="tpu_custom_call" | custom-call | tf_op jit(solution)/shard_map/spread/pallas_call | solution.py:365
  52.9 3.3 %copy.10 = f32[2,73,2048]{2,0,1:T(2,128)} copy(f32[2,73,2048]{2,1,0:T(8,128)} %spread.1) | data formatting | bytes 2392064 | tf_op jit(solution)/shard_map/spread/pallas_call | solution.py:365

commit v2 on v1

v2 whole, which is shorter than its diff:
```python
import jax
import jax.numpy as jnp
from jax import lax
from jax.experimental import pallas as pl
from jax.experimental.pallas import tpu as pltpu
from jax.sharding import PartitionSpec as P

STEPS = 2
SAMPLES = 73
HISTORY = 71
MOST = 16
EARLY = 18

drift = 0.2
moves = ((-1, -1), (-1, 0), (-1, 1), (0, -1), (0, 1), (1, -1), (1, 0), (1, 1))
MESH = pl.DeviceIdType.MESH
f32 = jnp.float32
bf16 = jnp.bfloat16
i32 = jnp.int32
NT = (((1,), (1,)), ((), ()))
TN = (((0,), (0,)), ((), ()))


def iota(shape, dim):
    return lax.broadcasted_iota(i32, shape, dim)


def halves(x):
    high = x.astype(bf16)
    return high, (x - high.astype(f32)).astype(bf16)


def dot(a, b, dims=(((1,), (0,)), ((), ()))):
    return lax.dot_general(a, b, dims, preferred_element_type=f32)


def swap_blocks(x):
    sub = iota((8, 128), 0)
    block = iota((8, 128), 1) // 16
    for b in (1, 2, 4):
        row_bit = (sub // b) % 2
        col_bit = (block // b) % 2
        down = pltpu.roll(pltpu.roll(x, b, 0), 128 - 16 * b, 1)
        up = pltpu.roll(pltpu.roll(x, 8 - b, 0), 16 * b, 1)
        x = jnp.where(row_bit > col_bit, down, jnp.where(row_bit < col_bit, up, x))
    return x


def lookup(table, index):
    held = jnp.minimum(jnp.maximum(index, 0), 127)
    parts = []
    for n in range(4):
        at = jnp.broadcast_to(held[:, 128 * n : 128 * n + 128], (8, 128))
        parts.append(jnp.take_along_axis(table, at, axis=1))
    return jnp.concatenate(parts, axis=1)


def advance_kernel(
    leavers_ref, velocity_hbm, start_ref, cells_ref, history_hbm, owner_ref, filter_ref,
    slabs_ref, late_ref, end_ref,
    velocity_ref, history_ref, planes, edges, edges_in, packed, packed_in, spots, spots_in, corners,
    chosen, split_main, split_tail, split_late, message, arrived, late, late_in, slabs,
    edge_send, edge_recv, packed_send, packed_recv, spot_send, spot_recv, send_sem, recv_sem, late_sems, own_sems,
    input_sems, slab_sems,
):
    ty = lax.axis_index("ty")
    tx = lax.axis_index("tx")
    me = ty * 16 + tx
    down = [lax.rem(ty + k, 8) for k in range(8)]
    along_x = [lax.rem(tx + k, 16) for k in range(16)]
    barrier = pltpu.get_barrier_semaphore()
    load_velocity = pltpu.make_async_copy(velocity_hbm, velocity_ref, input_sems.at[0])
    load_history = pltpu.make_async_copy(history_hbm, history_ref, input_sems.at[1])
    load_velocity.start()
    load_history.start()

    def greet(k, carry):
        row = lax.rem(ty + k, 8)
        for m in range(1, 16):
            pl.semaphore_signal(barrier, inc=1, device_id=(row, along_x[m]), device_id_type=MESH)
        return carry

    lax.fori_loop(0, 8, greet, 0)
    for k in range(1, 8):
        pl.semaphore_signal(barrier, inc=1, device_id=(down[k], tx), device_id_type=MESH)

    def cell_of(section):
        both = cells_ref[section]
        return both[0:1], both[1:2]

    def neighbour(j):
        dy, dx = moves[j]
        return (down[dy % 8], along_x[dx % 16])

    def history_of(c, n):
        return history_ref[pl.ds(2 * n + c, HISTORY, stride=8), :]

    counts = [leavers_ref[0, j] for j in range(8)]
    starts = [0]
    for j in range(8):
        starts.append(starts[j] + counts[j])
    place = iota((128, 128), 0) % 16
    way = iota((128, 128), 0) // 16
    first = jnp.zeros((128, 128), i32)
    many = jnp.zeros((128, 128), i32)
    for j in range(8):
        first = jnp.where(way == j, starts[j], first)
        many = jnp.where(way == j, counts[j], many)
    leaving = (iota((128, 128), 1) == first + place) & (place < many)
    leaving = jnp.where(leaving, 1.0, 0.0).astype(bf16)

    load_velocity.wait()
    for a in range(3):
        for c in range(2):
            high, low = halves(velocity_ref[c, a])
            planes[2 * a, 128 * c : 128 * c + 128, 0:128] = high
            planes[2 * a, 128 * c : 128 * c + 128, 128:256] = low
    pick_row = iota((8, 256), 0)
    pick_lane = iota((8, 256), 1) % 128
    pick = ((pick_lane == 0) & (pick_row == 0)) | ((pick_lane == 127) & (pick_row == 1))
    pick = jnp.where(pick, 1.0, 0.0).astype(bf16)
    for a in range(3):
        sides = dot(pick, planes[2 * a], NT)
        for c in range(2):
            r = 3 * c + a
            edges[0, r : r + 1, :] = velocity_ref[c, a, 0:1, :]
            edges[1, r : r + 1, :] = velocity_ref[c, a, 127:128, :]
            edges[2, r : r + 1, :] = sides[0:1, 128 * c : 128 * c + 128]
            edges[3, r : r + 1, :] = sides[1:2, 128 * c : 128 * c + 128]
    for kind in range(4):
        edges[kind, 6:8, :] = jnp.zeros((2, 128), f32)

    load_history.wait()
    for c in range(2):
        high, low = halves(history_of(c, 0))
        block = dot(leaving, high, NT) + dot(leaving, low, NT)
        packed[:, :, 128 * c : 128 * c + HISTORY] = block.reshape(8, 16, HISTORY)

    for a in range(2):
        for c in range(2):
            high, low = halves(0.5 * (velocity_ref[c, a] + velocity_ref[c, a + 1]))
            planes[2 * a + 1, 128 * c : 128 * c + 128, 0:128] = high
            planes[2 * a + 1, 128 * c : 128 * c + 128, 128:256] = low

    def gather(section, carry):
        plane = planes[2 * (section // 4) + (section % 4 + 1) // 2]
        cell_y, cell_x = cell_of(section)
        column = iota((256, 512), 0) % 128
        row = iota((128, 512), 0)
        for dx in range(2):
            here = jnp.where(column == cell_x + dx, 1.0, 0.0).astype(bf16)
            along = dot(plane, here)
            for dy in range(2):
                on = row == cell_y + dy
                for c in range(2):
                    part = jnp.where(on, along[128 * c : 128 * c + 128], 0.0)
                    at = 4 * dy + 2 * dx + c
                    corners[section, at : at + 1, :] = jnp.sum(part, axis=0, keepdims=True)
        return carry

    lax.fori_loop(0, 8, gather, 0)

    pl.semaphore_wait(barrier, 127)

    edge_copies = []
    packed_copies = []
    spot_copies = []
    for j in range(8):
        dy, dx = moves[j]
        kind = {1: 1, -1: 0}.get(dy, 3 if dx == 1 else 2)
        edge_copies.append(pltpu.make_async_remote_copy(
            src_ref=edges.at[kind], dst_ref=edges_in.at[j], send_sem=edge_send.at[j], recv_sem=edge_recv.at[j],
            device_id=neighbour(j), device_id_type=MESH))
        packed_copies.append(pltpu.make_async_remote_copy(
            src_ref=packed.at[j], dst_ref=packed_in.at[j], send_sem=packed_send.at[j], recv_sem=packed_recv.at[j],
            device_id=neighbour(j), device_id_type=MESH))
        spot_copies.append(pltpu.make_async_remote_copy(
            src_ref=spots, dst_ref=spots_in.at[j], send_sem=spot_send.at[j], recv_sem=spot_recv.at[j],
            device_id=neighbour(j), device_id_type=MESH))
    for copy in edge_copies:
        copy.start()
    for copy in packed_copies:
        copy.start()

    named = iota((128, 512), 0) == owner_ref[...]
    before = dot(
        jnp.where(named, 1.0, 0.0).astype(bf16),
        jnp.where(iota((512, 512), 0) < iota((512, 512), 1), 1.0, 0.0).astype(bf16))
    rank = jnp.sum(jnp.where(named, before, 0.0), axis=0, keepdims=True).astype(i32)
    target = owner_ref[...] * 16 + rank

    def choose(k, carry):
        place = target - lax.rem(ty + k, 8) * 256
        chosen[k] = jnp.where(iota((256, 512), 0) == place, 1.0, 0.0).astype(bf16)
        return carry

    lax.fori_loop(0, 8, choose, 0)

    matrix = filter_ref[...]

    def keep_filtered(low, lanes):
        for c in range(2):
            high, rest = halves(low[c][0:64])
            split_main[64 * c : 64 * c + 64, lanes] = high
            split_main[128 + 64 * c : 192 + 64 * c, lanes] = rest
        high, rest = halves(jnp.concatenate([low[0][64:72], low[1][64:72]], axis=0))
        split_tail[0:16, lanes] = high
        split_tail[16:32, lanes] = rest

    def filtered(series):
        return lax.dot_general(
            matrix[:, 0:HISTORY], series, (((1,), (0,)), ((), ())),
            precision=lax.Precision.HIGHEST, preferred_element_type=f32)

    staying = [filtered(jnp.concatenate([history_of(c, n) for n in range(1, 4)], axis=1)) for c in range(2)]
    keep_filtered(staying, slice(128, 512))

    for copy in edge_copies:
        copy.wait_recv()
    where_from = {move: j for j, move in enumerate(moves)}
    top = edges_in[where_from[(1, 0)]]
    bottom = edges_in[where_from[(-1, 0)]]
    left = edges_in[where_from[(0, 1)]]
    right = edges_in[where_from[(0, -1)]]
    top_left = edges_in[where_from[(1, 1)]][:, 127:128]
    top_right = edges_in[where_from[(1, -1)]][:, 0:1]
    bottom_left = edges_in[where_from[(-1, 1)]][:, 127:128]
    bottom_right = edges_in[where_from[(-1, -1)]][:, 0:1]

    def all_corners(section):
        step, part = section // 4, section % 4
        cell_y, cell_x = cell_of(section)
        sides = {}
        for dy in range(2):
            yy = cell_y + dy
            sides[dy] = (lookup(left, yy), lookup(right, yy))
        result = []
        ends = {}
        for dx in range(2):
            xx = cell_x + dx
            ends[dx] = tuple(
                jnp.where(xx < 0, lower, jnp.where(xx > 127, upper, lookup(line, xx)))
                for line, lower, upper in ((top, top_left, top_right), (bottom, bottom_left, bottom_right)))
        for dy in range(2):
            for dx in range(2):
                yy, xx = cell_y + dy, cell_x + dx
                outer = jnp.where(xx < 0, sides[dy][0], jnp.where(xx > 127, sides[dy][1], 0.0))
                outer = jnp.where(yy < 0, ends[dx][0], jnp.where(yy > 127, ends[dx][1], outer))
                rows = []
                for c in range(2):
                    a = step + (part == 3)
                    value = outer[3 * c + a : 3 * c + a + 1]
                    if part in (1, 2):
                        value = 0.5 * (value + outer[3 * c + a + 1 : 3 * c + a + 2])
                    rows.append(value)
                at = 4 * dy + 2 * dx
                result.append(corners[section, at : at + 2, :] + jnp.concatenate(rows, axis=0))
        return result

    def sample(section, held, point):
        cell_y, cell_x = cell_of(section)
        wy = point[0:1] - cell_y.astype(f32)
        wx = point[1:2] - cell_x.astype(f32)
        first_c, second_c, third_c, fourth_c = held
        return (1.0 - wy) * ((1.0 - wx) * first_c + wx * second_c) + wy * ((1.0 - wx) * third_c + wx * fourth_c)

    def rest_of_step(step, held, point, k_one):
        spot = point + 0.5 * drift * k_one
        k_two = sample(4 * step + 1, held[0], spot)
        spot = point + 0.5 * drift * k_two
        k_three = sample(4 * step + 2, held[1], spot)
        spot = point + drift * k_three
        k_four = sample(4 * step + 3, held[2], spot)
        return point + drift / 6.0 * (k_one + 2.0 * k_two + 2.0 * k_three + k_four)

    point = start_ref[...]
    k_first = sample(0, all_corners(0), point)
    point = rest_of_step(0, [all_corners(s) for s in (1, 2, 3)], point, k_first)

    spots[0:2, :] = point[:, 0:128]
    spots[2:4, :] = k_first[:, 0:128]
    spots[4:8, :] = jnp.zeros((4, 128), f32)
    for copy in spot_copies:
        copy.start()

    for copy in packed_copies:
        copy.wait_recv()
    lane = iota((1, 128), 1)
    changed = []
    for c in range(2):
        block = packed_in[:, :, 128 * c : 128 * c + HISTORY].reshape(128, HISTORY)
        high, low = halves(block)
        came = dot(high, leaving, TN) + dot(low, leaving, TN)
        changed.append(filtered(jnp.where(lane < starts[8], came, history_of(c, 0))))
    keep_filtered(changed, slice(0, 128))
    last_low = [jnp.concatenate([changed[c][72:73], staying[c][72:73]], axis=1) for c in range(2)]

    def deliver(k, carry):
        goal = lax.rem(ty + k, 8)
        pairs = dot(chosen[k], split_main[...], NT)
        message[pl.ds(16 * k, 16), 0:16, :] = (pairs[:, 0:128] + pairs[:, 128:256]).reshape(16, 16, 128)
        tail = dot(split_tail[...], chosen[k], NT)
        tail = tail[0:16] + tail[16:32]
        for h in range(2):
            for a in range(2):
                swapped = swap_blocks(tail[8 * a : 8 * a + 8, 128 * h : 128 * h + 128])
                message[pl.ds(16 * k + 8 * h, 8), 16 + a, :] = swapped

        def send(column):
            pltpu.make_async_remote_copy(
                src_ref=message.at[16 * k + column, pl.ds(0, EARLY)], dst_ref=arrived.at[me, pl.ds(0, EARLY)],
                send_sem=send_sem, recv_sem=recv_sem.at[k], device_id=(goal, column), device_id_type=MESH).start()

        for m in range(1, 16):
            send(along_x[m])

        @pl.when(k > 0)
        def _():
            send(tx)

        return carry

    lax.fori_loop(0, 8, deliver, 0)
    own_copy = pltpu.make_async_copy(message.at[tx, pl.ds(0, EARLY)], arrived.at[me, pl.ds(0, EARLY)], own_sems.at[0])
    own_copy.start()

    next_corners = all_corners(4)
    for copy in spot_copies:
        copy.wait_recv()
    moved_point = point[:, 0:128]
    moved_first = k_first[:, 0:128]
    for j in range(8):
        dy, dx = moves[j]
        here = (lane >= starts[j]) & (lane < starts[j + 1])
        arrival = spots_in[j]
        shift = jnp.where(iota((2, 128), 0) == 0, float(dy * 128), float(dx * 128))
        moved_point = jnp.where(here, arrival[0:2] - shift, moved_point)
        moved_first = jnp.where(here, arrival[2:4], moved_first)
    point = jnp.concatenate([moved_point, point[:, 128:512]], axis=1)
    k_first = jnp.concatenate([moved_first, k_first[:, 128:512]], axis=1)
    k_second = sample(4, next_corners, point)

    values = jnp.concatenate(last_low + [k_first, k_second, jnp.zeros((10, 512), f32)], axis=0)
    high, rest = halves(values)
    split_late[0:16, :] = high
    split_late[16:32, :] = rest

    def deliver_late(k, carry):
        goal = lax.rem(ty + k, 8)
        tail = dot(split_late[...], chosen[k], NT)
        tail = tail[0:8] + tail[16:24]
        for h in range(2):
            late[pl.ds(16 * k + 8 * h, 8), 0, :] = swap_blocks(tail[:, 128 * h : 128 * h + 128])

        def send(column):
            pltpu.make_async_remote_copy(
                src_ref=late.at[16 * k + column], dst_ref=late_in.at[me],
                send_sem=late_sems.at[0], recv_sem=late_sems.at[1], device_id=(goal, column),
                device_id_type=MESH).start()

        for m in range(1, 16):
            send(along_x[m])

        @pl.when(k > 0)
        def _():
            send(tx)

        return carry

    lax.fori_loop(0, 8, deliver_late, 0)
    own_late = pltpu.make_async_copy(late.at[tx], late_in.at[me], own_sems.at[1])
    own_late.start()

    end_ref[...] = rest_of_step(1, [all_corners(s) for s in (5, 6, 7)], point, k_second)

    def place_row(k, carry):
        sender = lax.rem(ty - k + 8, 8)

        @pl.when(k == 0)
        def _():
            landed = arrived.at[pl.ds(0, 15), pl.ds(0, EARLY)]
            pltpu.make_async_copy(landed, landed, recv_sem.at[0]).wait()
            own_copy.wait()

        @pl.when(k > 0)
        def _():
            landed = arrived.at[pl.ds(0, 16), pl.ds(0, EARLY)]
            pltpu.make_async_copy(landed, landed, recv_sem.at[k]).wait()

        slab = slabs.at[k]
        for h in range(2):
            tiles = pl.ds(sender * 16 + 8 * h, 8)
            wide = jnp.transpose(arrived[tiles, 0:16, :].reshape(128, 128))
            for c in range(2):
                slab[pl.ds(2 * h + c, 64, stride=4), :] = wide[64 * c : 64 * c + 64]
                slab[pl.ds(64 * 4 + 2 * h + c, 8, stride=4), :] = swap_blocks(arrived[tiles, 16 + c, :])
        pltpu.make_async_copy(slabs.at[k], slabs_ref.at[sender], slab_sems.at[k]).start()
        return carry

    lax.fori_loop(0, 8, place_row, 0)

    for copy in edge_copies + packed_copies + spot_copies:
        copy.wait_send()
    own_late.wait()
    sent = message.at[pl.ds(0, 127), pl.ds(0, EARLY)]
    pltpu.make_async_copy(sent, sent, send_sem).wait()
    sent = late.at[pl.ds(0, 127)]
    pltpu.make_async_copy(sent, sent, late_sems.at[0]).wait()
    pltpu.make_async_copy(sent, sent, late_sems.at[1]).wait()
    for block in range(16):
        part = swap_blocks(late_in[8 * block : 8 * block + 8, 0, :])
        for kind in range(3):
            late_ref[kind, 2 * block : 2 * block + 2, :] = part[2 * kind : 2 * kind + 2]
    for k in range(8):
        pltpu.make_async_copy(slabs.at[k], slabs_ref.at[lax.rem(ty - k + 8, 8)], slab_sems.at[k]).wait()


def finish_kernel(slabs_ref, late_ref, filter_ref, out_ref):
    rows = out_ref.reshape(SAMPLES * 8, 128)
    matrix = filter_ref[...]
    weights = [jnp.broadcast_to(matrix[:, at : at + 1], (SAMPLES, 128)) for at in (HISTORY, HISTORY + 1)]
    for s in range(2):
        for r in range(4):
            at = 4 * s + r
            early = slabs_ref[s, pl.ds(r, SAMPLES - 1, stride=4), :]
            low = jnp.concatenate([early, late_ref[0, at : at + 1, :]], axis=0)
            first, second = late_ref[1, at : at + 1, :], late_ref[2, at : at + 1, :]
            rows[pl.ds(at, SAMPLES, stride=8), :] = low + weights[0] * first + weights[1] * second


def per_device(velocity, start_position, cells, history, leavers, owner, filter_matrix):
    vmem = pl.BlockSpec(memory_space=pltpu.VMEM)
    hbm = pl.BlockSpec(memory_space=pl.ANY)
    slabs, late, end = pl.pallas_call(
        advance_kernel,
        out_shape=(
            jax.ShapeDtypeStruct((8, 288, 128), f32),
            jax.ShapeDtypeStruct((3, 32, 128), f32),
            jax.ShapeDtypeStruct((2, 512), f32),
        ),
        in_specs=[pl.BlockSpec(memory_space=pltpu.SMEM), hbm, vmem, vmem, hbm, vmem, vmem],
        out_specs=(hbm, vmem, vmem),
        scratch_shapes=[
            pltpu.VMEM((2, 3, 128, 128), f32),
            pltpu.VMEM((HISTORY * 8, 128), f32),
            pltpu.VMEM((5, 256, 256), bf16),
            pltpu.VMEM((4, 8, 128), f32),
            pltpu.VMEM((8, 8, 128), f32),
            pltpu.VMEM((8, 16, 256), f32),
            pltpu.VMEM((8, 16, 256), f32),
            pltpu.VMEM((8, 128), f32),
            pltpu.VMEM((8, 8, 128), f32),
            pltpu.VMEM((8, 8, 512), f32),
            pltpu.VMEM((8, 256, 512), bf16),
            pltpu.VMEM((256, 512), bf16),
            pltpu.VMEM((32, 512), bf16),
            pltpu.VMEM((32, 512), bf16),
            pltpu.VMEM((128, 24, 128), f32),
            pltpu.VMEM((128, 24, 128), f32),
            pltpu.VMEM((128, 1, 128), f32),
            pltpu.VMEM((128, 1, 128), f32),
            pltpu.VMEM((8, 288, 128), f32),
        ]
        + [pltpu.SemaphoreType.DMA((8,))] * 6
        + [
            pltpu.SemaphoreType.DMA,
            pltpu.SemaphoreType.DMA((8,)),
            pltpu.SemaphoreType.DMA((2,)),
            pltpu.SemaphoreType.DMA((2,)),
            pltpu.SemaphoreType.DMA((2,)),
            pltpu.SemaphoreType.DMA((8,)),
        ],
        compiler_params=pltpu.CompilerParams(collective_id=0, has_side_effects=True),
        name="advance",
    )(
        leavers, velocity, start_position, cells.reshape(8, 2, 512),
        history.reshape(2, HISTORY, 4, 128).transpose(1, 2, 0, 3).reshape(HISTORY * 8, 128),
        owner.reshape(1, 512), filter_matrix,
    )
    out = pl.pallas_call(
        finish_kernel,
        grid=(4,),
        out_shape=jax.ShapeDtypeStruct((SAMPLES, 32, 128), f32),
        in_specs=[
            pl.BlockSpec((2, 288, 128), lambda i: (i, 0, 0)),
            pl.BlockSpec((3, 8, 128), lambda i: (0, i, 0)),
            pl.BlockSpec((SAMPLES, SAMPLES), lambda i: (0, 0)),
        ],
        out_specs=pl.BlockSpec((SAMPLES, 8, 128), lambda i: (0, i, 0)),
        name="finish",
    )(slabs, late, filter_matrix)
    return out.reshape(SAMPLES, 16, 2, 128).transpose(2, 0, 1, 3).reshape(2, SAMPLES, 2048)


def solution(mesh):
    placed = (
        P(None, None, "ty", "tx"),
        P(None, ("ty", "tx")),
        P(None, None, None, ("ty", "tx")),
        P(None, None, ("ty", "tx")),
        P(),
        P(("ty", "tx"), None),
        P(),
    )
    return jax.shard_map(
        per_device,
        mesh=mesh,
        in_specs=placed,
        out_specs=P(None, None, ("ty", "tx")),
        check_vma=False,
    )
```

time: 56.6 us -> 41.9 us (0.74)
  local copies, waits for them, and re-layouts: 7.94 us -> 0 us
  Pallas kernels: 48.2 us -> 41.6 us
    pallas_call x2, Pallas kernels: 48.2 us -> 41.6 us  [the longest x1 38 us: per_device(): pl.pallas_call(advance_kernel, out_shape=(jax.ShapeDtypeStruct((8, 288, 1...]
    unnamed x2 -> x0, local copies, waits for them, and re-layouts: 3.27 us -> none
    pallas_call x1 -> x0, local copies, waits for them, and re-layouts: 3.26 us -> none  [per_device(): pl.pallas_call(spread_kernel, grid=(8,), out_shape=jax.ShapeDtypeStruct((...]
    reshape x1 -> x0, local copies, waits for them, and re-layouts: 1.42 us -> none  [per_device(): cells.reshape(16, 1, 512)]
where the time goes in v2:
time: 41.9 us; the launch traced here: 41.6 us
  Pallas kernels  41.6 us (99%)
    pallas_call x1, Pallas kernels, per_device(): pl.pallas_call(advance_kernel, out_shape=(jax.ShapeDtypeStruct((8, 288, 1...  38 us
    pallas_call x1, Pallas kernels, per_device(): pl.pallas_call(finish_kernel, grid=(4,), out_shape=jax.ShapeDtypeStruct((...  3.67 us

profile of v2, /device:TPU:1, one launch (start us, length us, event | category | flops | bytes accessed | tf_op | source)
XLA Modules:
  0.0 41.6 jit_solution(13318197900283981149)
XLA Ops:
  0.0 38.0 %advance.1 = (f32[8,288,128]{2,1,0:T(8,128)}, f32[3,32,128]{2,1,0:T(8,128)}, f32[2,512]{1,0:T(2,128)}) custom-call(s32[1,8]{1,0:T(1,128)} %leavers_ref.1, f32[2,3,128,128]{3,2,1,0:T(8,128)} %velocity_hbm.1, f32[2,512]{1,0:T(2,128)} %start_ref.1, s32[8,2,512]{2,1,0:T(2,128)} %bitcast.13, f32[568,128]{1,0:T(8,128)} %bitcast.12, s32[1,512]{1,0:T(1,128)} %bitcast.14, ...), custom_call_target="tpu_custom_call" | custom-call | tf_op jit(solution)/shard_map/advance/pallas_call | solution.py:434
  38.0 3.7 %finish.1 = f32[73,32,128]{2,1,0:T(8,128)} custom-call(f32[8,288,128]{2,1,0:T(8,128)} %get-tuple-element.7.slabs_ref, f32[3,32,128]{2,1,0:T(8,128)} %get-tuple-element.8.late_ref, f32[73,73]{1,0:T(8,128)} %filter_ref.3), custom_call_target="tpu_custom_call" | custom-call | tf_op jit(solution)/shard_map/finish/pallas_call | solution.py:480

commit v3 on v2

--- a/solution.py
+++ b/solution.py
@@ -10,6 +10,8 @@
 HISTORY = 71
 MOST = 16
 EARLY = 18
+SPLIT = 6
+STRIDE = 5
 
 drift = 0.2
 moves = ((-1, -1), (-1, 0), (-1, 1), (0, -1), (0, 1), (1, -1), (1, 0), (1, 1))
@@ -59,9 +61,9 @@
     leavers_ref, velocity_hbm, start_ref, cells_ref, history_hbm, owner_ref, filter_ref,
     slabs_ref, late_ref, end_ref,
     velocity_ref, history_ref, planes, edges, edges_in, packed, packed_in, spots, spots_in, corners,
-    chosen, split_main, split_tail, split_late, message, arrived, late, late_in, slabs,
-    edge_send, edge_recv, packed_send, packed_recv, spot_send, spot_recv, send_sem, recv_sem, late_sems, own_sems,
-    input_sems, slab_sems,
+    chosen, split_main, split_tail, split_late, message, arrived, late, late_in,
+    edge_send, edge_recv, packed_send, packed_recv, spot_send, spot_recv, send_sems, recv_sem, late_sems, own_sems,
+    input_sems, column_in,
 ):
     ty = lax.axis_index("ty")
     tx = lax.axis_index("tx")
@@ -74,15 +76,9 @@
     load_velocity.start()
     load_history.start()
 
-    def greet(k, carry):
-        row = lax.rem(ty + k, 8)
-        for m in range(1, 16):
-            pl.semaphore_signal(barrier, inc=1, device_id=(row, along_x[m]), device_id_type=MESH)
-        return carry
-
-    lax.fori_loop(0, 8, greet, 0)
-    for k in range(1, 8):
-        pl.semaphore_signal(barrier, inc=1, device_id=(down[k], tx), device_id_type=MESH)
+    close = [(0, m) for m in range(1, 16)] + [(k, 0) for k in range(1, 8)] + [(1, 1), (1, 15), (7, 1), (7, 15)]
+    for k, m in close:
+        pl.semaphore_signal(barrier, inc=1, device_id=(down[k], along_x[m]), device_id_type=MESH)
 
     def cell_of(section):
         both = cells_ref[section]
@@ -158,9 +154,11 @@
                     corners[section, at : at + 1, :] = jnp.sum(part, axis=0, keepdims=True)
         return carry
 
-    lax.fori_loop(0, 8, gather, 0)
-
-    pl.semaphore_wait(barrier, 127)
+    lax.fori_loop(0, 4, gather, 0)
+
+    pl.semaphore_wait(barrier, len(close))
+    for m in range(1, 16):
+        pl.semaphore_signal(column_in, inc=1, device_id=(ty, along_x[m]), device_id_type=MESH)
 
     edge_copies = []
     packed_copies = []
@@ -188,13 +186,6 @@
         jnp.where(iota((512, 512), 0) < iota((512, 512), 1), 1.0, 0.0).astype(bf16))
     rank = jnp.sum(jnp.where(named, before, 0.0), axis=0, keepdims=True).astype(i32)
     target = owner_ref[...] * 16 + rank
-
-    def choose(k, carry):
-        place = target - lax.rem(ty + k, 8) * 256
-        chosen[k] = jnp.where(iota((256, 512), 0) == place, 1.0, 0.0).astype(bf16)
-        return carry
-
-    lax.fori_loop(0, 8, choose, 0)
 
     matrix = filter_ref[...]
 
@@ -295,35 +286,53 @@
     keep_filtered(changed, slice(0, 128))
     last_low = [jnp.concatenate([changed[c][72:73], staying[c][72:73]], axis=1) for c in range(2)]
 
-    def deliver(k, carry):
-        goal = lax.rem(ty + k, 8)
-        pairs = dot(chosen[k], split_main[...], NT)
+    def fill(k):
+        place = target - lax.rem(ty + STRIDE * k, 8) * 256
+        here = jnp.where(iota((256, 512), 0) == place, 1.0, 0.0).astype(bf16)
+        pairs = dot(here, split_main[...], NT)
         message[pl.ds(16 * k, 16), 0:16, :] = (pairs[:, 0:128] + pairs[:, 128:256]).reshape(16, 16, 128)
-        tail = dot(split_tail[...], chosen[k], NT)
+        tail = dot(split_tail[...], here, NT)
         tail = tail[0:16] + tail[16:32]
         for h in range(2):
             for a in range(2):
                 swapped = swap_blocks(tail[8 * a : 8 * a + 8, 128 * h : 128 * h + 128])
                 message[pl.ds(16 * k + 8 * h, 8), 16 + a, :] = swapped
-
-        def send(column):
-            pltpu.make_async_remote_copy(
-                src_ref=message.at[16 * k + column, pl.ds(0, EARLY)], dst_ref=arrived.at[me, pl.ds(0, EARLY)],
-                send_sem=send_sem, recv_sem=recv_sem.at[k], device_id=(goal, column), device_id_type=MESH).start()
-
+        return here
+
+    def newest(here):
+        tail = dot(split_late[...], here, NT)
+        tail = tail[0:8] + tail[16:24]
+        return [swap_blocks(tail[:, 128 * h : 128 * h + 128]) for h in range(2)]
+
+    def send_row(k, copy_to):
+        goal = lax.rem(ty + STRIDE * k, 8)
         for m in range(1, 16):
-            send(along_x[m])
+            copy_to(goal, along_x[m]).start()
 
         @pl.when(k > 0)
         def _():
-            send(tx)
-
+            copy_to(goal, tx).start()
+
+    def bulk(k, rows):
+        def copy_to(goal, column):
+            return pltpu.make_async_remote_copy(
+                src_ref=message.at[16 * k + column, pl.ds(0, rows)], dst_ref=arrived.at[me, pl.ds(0, rows)],
+                send_sem=send_sems.at[rows - EARLY], recv_sem=recv_sem.at[k], device_id=(goal, column),
+                device_id_type=MESH)
+
+        return copy_to
+
+    def deliver(k, carry):
+        chosen[k] = fill(k)
+        send_row(k, bulk(k, EARLY))
         return carry
 
-    lax.fori_loop(0, 8, deliver, 0)
+    pl.semaphore_wait(column_in, 15)
+    lax.fori_loop(0, SPLIT, deliver, 0)
     own_copy = pltpu.make_async_copy(message.at[tx, pl.ds(0, EARLY)], arrived.at[me, pl.ds(0, EARLY)], own_sems.at[0])
     own_copy.start()
 
+    lax.fori_loop(4, 8, gather, 0)
     next_corners = all_corners(4)
     for copy in spot_copies:
         copy.wait_recv()
@@ -346,86 +355,102 @@
     split_late[16:32, :] = rest
 
     def deliver_late(k, carry):
-        goal = lax.rem(ty + k, 8)
-        tail = dot(split_late[...], chosen[k], NT)
-        tail = tail[0:8] + tail[16:24]
+        parts = newest(chosen[k])
         for h in range(2):
-            late[pl.ds(16 * k + 8 * h, 8), 0, :] = swap_blocks(tail[:, 128 * h : 128 * h + 128])
-
-        def send(column):
-            pltpu.make_async_remote_copy(
-                src_ref=late.at[16 * k + column], dst_ref=late_in.at[me],
-                send_sem=late_sems.at[0], recv_sem=late_sems.at[1], device_id=(goal, column),
-                device_id_type=MESH).start()
-
-        for m in range(1, 16):
-            send(along_x[m])
-
-        @pl.when(k > 0)
-        def _():
-            send(tx)
-
+            late[pl.ds(16 * k + 8 * h, 8), 0, :] = parts[h]
+
+        def copy_to(goal, column):
+            return pltpu.make_async_remote_copy(
+                src_ref=late.at[16 * k + column], dst_ref=late_in.at[me], send_sem=late_sems.at[0],
+                recv_sem=late_sems.at[1], device_id=(goal, column), device_id_type=MESH)
+
+        send_row(k, copy_to)
         return carry
 
-    lax.fori_loop(0, 8, deliver_late, 0)
+    lax.fori_loop(0, SPLIT, deliver_late, 0)
+
+    def deliver_all(k, carry):
+        parts = newest(fill(k))
+        for h in range(2):
+            message[pl.ds(16 * k + 8 * h, 8), EARLY, :] = parts[h]
+        send_row(k, bulk(k, EARLY + 1))
+        return carry
+
+    lax.fori_loop(SPLIT, 8, deliver_all, 0)
     own_late = pltpu.make_async_copy(late.at[tx], late_in.at[me], own_sems.at[1])
     own_late.start()
 
     end_ref[...] = rest_of_step(1, [all_corners(s) for s in (5, 6, 7)], point, k_second)
 
+    def landed(number, rows):
+        return arrived.at[pl.ds(0, number), pl.ds(0, rows)]
+
+    def keep_late(sender, h, part):
+        part = swap_blocks(part)
+        for kind in range(3):
+            late_ref[kind, sender, 2 * h : 2 * h + 2, :] = part[2 * kind : 2 * kind + 2]
+
     def place_row(k, carry):
-        sender = lax.rem(ty - k + 8, 8)
+        sender = lax.rem(ty - STRIDE * k + 64, 8)
 
         @pl.when(k == 0)
         def _():
-            landed = arrived.at[pl.ds(0, 15), pl.ds(0, EARLY)]
-            pltpu.make_async_copy(landed, landed, recv_sem.at[0]).wait()
+            pltpu.make_async_copy(landed(15, EARLY), landed(15, EARLY), recv_sem.at[0]).wait()
             own_copy.wait()
 
-        @pl.when(k > 0)
+        @pl.when((k > 0) & (k < SPLIT))
         def _():
-            landed = arrived.at[pl.ds(0, 16), pl.ds(0, EARLY)]
-            pltpu.make_async_copy(landed, landed, recv_sem.at[k]).wait()
-
-        slab = slabs.at[k]
+            pltpu.make_async_copy(landed(16, EARLY), landed(16, EARLY), recv_sem.at[k]).wait()
+
+        @pl.when(k >= SPLIT)
+        def _():
+            pltpu.make_async_copy(landed(16, EARLY + 1), landed(16, EARLY + 1), recv_sem.at[k]).wait()
+            for h in range(2):
+                keep_late(sender, h, arrived[pl.ds(sender * 16 + 8 * h, 8), EARLY, :])
+
+        slab = slabs_ref.at[sender]
         for h in range(2):
             tiles = pl.ds(sender * 16 + 8 * h, 8)
             wide = jnp.transpose(arrived[tiles, 0:16, :].reshape(128, 128))
             for c in range(2):
                 slab[pl.ds(2 * h + c, 64, stride=4), :] = wide[64 * c : 64 * c + 64]
                 slab[pl.ds(64 * 4 + 2 * h + c, 8, stride=4), :] = swap_blocks(arrived[tiles, 16 + c, :])
-        pltpu.make_async_copy(slabs.at[k], slabs_ref.at[sender], slab_sems.at[k]).start()
         return carry
 
     lax.fori_loop(0, 8, place_row, 0)
 
+    own_late.wait()
+    few = 16 * SPLIT - 1
+    sent = late.at[pl.ds(0, few)]
+    pltpu.make_async_copy(sent, sent, late_sems.at[1]).wait()
+    for k in range(SPLIT):
+        sender = lax.rem(ty - STRIDE * k + 64, 8)
+        for h in range(2):
+            keep_late(sender, h, late_in[pl.ds(sender * 16 + 8 * h, 8), 0, :])
     for copy in edge_copies + packed_copies + spot_copies:
         copy.wait_send()
-    own_late.wait()
-    sent = message.at[pl.ds(0, 127), pl.ds(0, EARLY)]
-    pltpu.make_async_copy(sent, sent, send_sem).wait()
-    sent = late.at[pl.ds(0, 127)]
     pltpu.make_async_copy(sent, sent, late_sems.at[0]).wait()
-    pltpu.make_async_copy(sent, sent, late_sems.at[1]).wait()
-    for block in range(16):
-        part = swap_blocks(late_in[8 * block : 8 * block + 8, 0, :])
-        for kind in range(3):
-            late_ref[kind, 2 * block : 2 * block + 2, :] = part[2 * kind : 2 * kind + 2]
-    for k in range(8):
-        pltpu.make_async_copy(slabs.at[k], slabs_ref.at[lax.rem(ty - k + 8, 8)], slab_sems.at[k]).wait()
-
-
-def finish_kernel(slabs_ref, late_ref, filter_ref, out_ref):
-    rows = out_ref.reshape(SAMPLES * 8, 128)
+    pltpu.make_async_copy(landed(few, EARLY), landed(few, EARLY), send_sems.at[0]).wait()
+    rest = 128 - 16 * SPLIT
+    pltpu.make_async_copy(landed(rest, EARLY + 1), landed(rest, EARLY + 1), send_sems.at[1]).wait()
+
+
+def finish_kernel(slabs_ref, late_ref, filter_ref, out_ref, buffer, sems):
     matrix = filter_ref[...]
     weights = [jnp.broadcast_to(matrix[:, at : at + 1], (SAMPLES, 128)) for at in (HISTORY, HISTORY + 1)]
-    for s in range(2):
-        for r in range(4):
-            at = 4 * s + r
-            early = slabs_ref[s, pl.ds(r, SAMPLES - 1, stride=4), :]
-            low = jnp.concatenate([early, late_ref[0, at : at + 1, :]], axis=0)
-            first, second = late_ref[1, at : at + 1, :], late_ref[2, at : at + 1, :]
-            rows[pl.ds(at, SAMPLES, stride=8), :] = low + weights[0] * first + weights[1] * second
+    copies = []
+    for part in range(4):
+        rows = buffer.at[part].reshape(SAMPLES * 8, 128)
+        for r in range(8):
+            at = 8 * part + r
+            early = slabs_ref[at // 4, pl.ds(at % 4, SAMPLES - 1, stride=4), :]
+            low = jnp.concatenate([early, late_ref[0, at // 4, at % 4 : at % 4 + 1, :]], axis=0)
+            first, second = (late_ref[kind, at // 4, at % 4 : at % 4 + 1, :] for kind in (1, 2))
+            rows[pl.ds(r, SAMPLES, stride=8), :] = low + weights[0] * first + weights[1] * second
+        copies.append(pltpu.make_async_copy(buffer.at[part], out_ref.at[:, pl.ds(8 * part, 8), :], sems.at[part]))
+        copies[-1].start()
+    for copy in copies:
+        copy.wait()
 
 
 def per_device(velocity, start_position, cells, history, leavers, owner, filter_matrix):
@@ -434,12 +459,12 @@
     slabs, late, end = pl.pallas_call(
         advance_kernel,
         out_shape=(
-            jax.ShapeDtypeStruct((8, 288, 128), f32),
-            jax.ShapeDtypeStruct((3, 32, 128), f32),
+            pltpu.VMEM((8, 288, 128), f32),
+            pltpu.VMEM((3, 8, 4, 128), f32),
             jax.ShapeDtypeStruct((2, 512), f32),
         ),
         in_specs=[pl.BlockSpec(memory_space=pltpu.SMEM), hbm, vmem, vmem, hbm, vmem, vmem],
-        out_specs=(hbm, vmem, vmem),
+        out_specs=(vmem, vmem, vmem),
         scratch_shapes=[
             pltpu.VMEM((2, 3, 128, 128), f32),
             pltpu.VMEM((HISTORY * 8, 128), f32),
@@ -451,24 +476,23 @@
             pltpu.VMEM((8, 128), f32),
             pltpu.VMEM((8, 8, 128), f32),
             pltpu.VMEM((8, 8, 512), f32),
-            pltpu.VMEM((8, 256, 512), bf16),
+            pltpu.VMEM((SPLIT, 256, 512), bf16),
             pltpu.VMEM((256, 512), bf16),
             pltpu.VMEM((32, 512), bf16),
             pltpu.VMEM((32, 512), bf16),
             pltpu.VMEM((128, 24, 128), f32),
             pltpu.VMEM((128, 24, 128), f32),
+            pltpu.VMEM((16 * SPLIT, 1, 128), f32),
             pltpu.VMEM((128, 1, 128), f32),
-            pltpu.VMEM((128, 1, 128), f32),
-            pltpu.VMEM((8, 288, 128), f32),
         ]
         + [pltpu.SemaphoreType.DMA((8,))] * 6
         + [
-            pltpu.SemaphoreType.DMA,
+            pltpu.SemaphoreType.DMA((2,)),
             pltpu.SemaphoreType.DMA((8,)),
             pltpu.SemaphoreType.DMA((2,)),
             pltpu.SemaphoreType.DMA((2,)),
             pltpu.SemaphoreType.DMA((2,)),
-            pltpu.SemaphoreType.DMA((8,)),
+            pltpu.SemaphoreType.REGULAR,
         ],
         compiler_params=pltpu.CompilerParams(collective_id=0, has_side_effects=True),
         name="advance",
@@ -479,16 +503,16 @@
     )
     out = pl.pallas_call(
         finish_kernel,
-        grid=(4,),
         out_shape=jax.ShapeDtypeStruct((SAMPLES, 32, 128), f32),
-        in_specs=[
-            pl.BlockSpec((2, 288, 128), lambda i: (i, 0, 0)),
-            pl.BlockSpec((3, 8, 128), lambda i: (0, i, 0)),
-            pl.BlockSpec((SAMPLES, SAMPLES), lambda i: (0, 0)),
-        ],
-        out_specs=pl.BlockSpec((SAMPLES, 8, 128), lambda i: (0, i, 0)),
+        in_specs=[vmem, vmem, vmem],
+        out_specs=hbm,
+        scratch_shapes=[pltpu.VMEM((4, SAMPLES, 8, 128), f32), pltpu.SemaphoreType.DMA((4,))],
         name="finish",
-    )(slabs, late, filter_matrix)
+    )(
+        pltpu.with_memory_space_constraint(slabs, pltpu.VMEM),
+        pltpu.with_memory_space_constraint(late, pltpu.VMEM),
+        filter_matrix,
+    )
     return out.reshape(SAMPLES, 16, 2, 128).transpose(2, 0, 1, 3).reshape(2, SAMPLES, 2048)
 
 

time: 41.9 us -> 37.2 us (0.89)
  Pallas kernels: 41.6 us -> 36.9 us
    pallas_call x2, Pallas kernels: 41.6 us -> 36.9 us  [the longest x1 34.8 us: per_device(): pl.pallas_call(advance_kernel, out_shape=(pltpu.VMEM((8, 288, 128), f32),...]
where the time goes in v3:
time: 37.2 us; the launch traced here: 36.9 us
  Pallas kernels  36.9 us (99%)
    pallas_call x1, Pallas kernels, per_device(): pl.pallas_call(advance_kernel, out_shape=(pltpu.VMEM((8, 288, 128), f32),...  34.8 us
    pallas_call x1, Pallas kernels, per_device(): pl.pallas_call(finish_kernel, out_shape=jax.ShapeDtypeStruct((SAMPLES, 32...  2.11 us

profile of v3, /device:TPU:1, one launch (start us, length us, event | category | flops | bytes accessed | tf_op | source)
XLA Modules:
  0.0 36.9 jit_solution(661774457485113213)
XLA Ops:
  0.0 34.8 %advance.1 = (f32[8,288,128]{2,1,0:T(8,128)S(1)}, f32[3,8,4,128]{3,2,1,0:T(4,128)S(1)}, f32[2,512]{1,0:T(2,128)}) custom-call(s32[1,8]{1,0:T(1,128)} %leavers_ref.1, f32[2,3,128,128]{3,2,1,0:T(8,128)} %velocity_hbm.1, f32[2,512]{1,0:T(2,128)} %start_ref.1, s32[8,2,512]{2,1,0:T(2,128)} %bitcast.13, f32[568,128]{1,0:T(8,128)} %bitcast.12, s32[1,512]{1,0:T(1,128)} %bitcast.14, ...), custom_call_target="tpu_custom_call" | custom-call | tf_op jit(solution)/shard_map/advance/pallas_call | solution.py:459
  34.8 2.1 %finish.1 = f32[73,32,128]{2,1,0:T(8,128)} custom-call(f32[8,288,128]{2,1,0:T(8,128)S(1)} %get-tuple-element.7.slabs_ref, f32[3,8,4,128]{3,2,1,0:T(4,128)S(1)} %get-tuple-element.8.late_ref, f32[73,73]{1,0:T(8,128)} %filter_ref.3), custom_call_target="tpu_custom_call" | custom-call | tf_op jit(solution)/shard_map/finish/pallas_call | solution.py:504

commit v4 on v3

--- a/solution.py
+++ b/solution.py
@@ -11,8 +11,6 @@
 MOST = 16
 EARLY = 18
 SPLIT = 6
-STRIDE = 5
-
 drift = 0.2
 moves = ((-1, -1), (-1, 0), (-1, 1), (0, -1), (0, 1), (1, -1), (1, 0), (1, 1))
 MESH = pl.DeviceIdType.MESH
@@ -34,6 +32,12 @@
 
 def dot(a, b, dims=(((1,), (0,)), ((), ()))):
     return lax.dot_general(a, b, dims, preferred_element_type=f32)
+
+
+def offset(k):
+    if isinstance(k, int):
+        return 5 * k % 8
+    return lax.rem(5 * k, 8)
 
 
 def swap_blocks(x):
@@ -61,7 +65,7 @@
     leavers_ref, velocity_hbm, start_ref, cells_ref, history_hbm, owner_ref, filter_ref,
     slabs_ref, late_ref, end_ref,
     velocity_ref, history_ref, planes, edges, edges_in, packed, packed_in, spots, spots_in, corners,
-    chosen, split_main, split_tail, split_late, message, arrived, late, late_in,
+    chosen, standing, split_main, split_tail, split_late, message, arrived, late, late_in,
     edge_send, edge_recv, packed_send, packed_recv, spot_send, spot_recv, send_sems, recv_sem, late_sems, own_sems,
     input_sems, column_in,
 ):
@@ -186,14 +190,19 @@
         jnp.where(iota((512, 512), 0) < iota((512, 512), 1), 1.0, 0.0).astype(bf16))
     rank = jnp.sum(jnp.where(named, before, 0.0), axis=0, keepdims=True).astype(i32)
     target = owner_ref[...] * 16 + rank
+    for n in range(4):
+        spread = jnp.broadcast_to(target[:, 128 * n : 128 * n + 128].astype(f32), (128, 128))
+        standing[128 * n : 128 * n + 128, :] = jnp.transpose(spread).astype(i32)
 
     matrix = filter_ref[...]
 
     def keep_filtered(low, lanes):
-        for c in range(2):
-            high, rest = halves(low[c][0:64])
-            split_main[64 * c : 64 * c + 64, lanes] = high
-            split_main[128 + 64 * c : 192 + 64 * c, lanes] = rest
+        main = jnp.concatenate([low[0][0:64], low[1][0:64]], axis=0)
+        for n in range(main.shape[1] // 128):
+            at = lanes.start + 128 * n
+            high, rest = halves(jnp.transpose(main[:, 128 * n : 128 * n + 128]))
+            split_main[at : at + 128, 0:128] = high
+            split_main[at : at + 128, 128:256] = rest
         high, rest = halves(jnp.concatenate([low[0][64:72], low[1][64:72]], axis=0))
         split_tail[0:16, lanes] = high
         split_tail[16:32, lanes] = rest
@@ -286,49 +295,57 @@
     keep_filtered(changed, slice(0, 128))
     last_low = [jnp.concatenate([changed[c][72:73], staying[c][72:73]], axis=1) for c in range(2)]
 
+    def goal_of(k):
+        return lax.rem(ty + offset(k), 8)
+
     def fill(k):
-        place = target - lax.rem(ty + STRIDE * k, 8) * 256
-        here = jnp.where(iota((256, 512), 0) == place, 1.0, 0.0).astype(bf16)
-        pairs = dot(here, split_main[...], NT)
+        first_column = goal_of(k) * 256
+        here = jnp.where(iota((256, 512), 0) == target - first_column, 1.0, 0.0).astype(bf16)
+        away = standing[...] - first_column
+        across = jnp.concatenate(
+            [jnp.where(iota((512, 128), 1) == away - 128 * h, 1.0, 0.0) for h in range(2)], axis=1).astype(bf16)
+        pairs = dot(here, split_main[...])
         message[pl.ds(16 * k, 16), 0:16, :] = (pairs[:, 0:128] + pairs[:, 128:256]).reshape(16, 16, 128)
-        tail = dot(split_tail[...], here, NT)
+        tail = dot(split_tail[...], across)
         tail = tail[0:16] + tail[16:32]
         for h in range(2):
             for a in range(2):
                 swapped = swap_blocks(tail[8 * a : 8 * a + 8, 128 * h : 128 * h + 128])
                 message[pl.ds(16 * k + 8 * h, 8), 16 + a, :] = swapped
-        return here
-
-    def newest(here):
-        tail = dot(split_late[...], here, NT)
+        return across
+
+    def newest(across):
+        tail = dot(split_late[...], across)
         tail = tail[0:8] + tail[16:24]
         return [swap_blocks(tail[:, 128 * h : 128 * h + 128]) for h in range(2)]
 
-    def send_row(k, copy_to):
-        goal = lax.rem(ty + STRIDE * k, 8)
+    def send_rows(rows, copy_of):
         for m in range(1, 16):
-            copy_to(goal, along_x[m]).start()
-
-        @pl.when(k > 0)
-        def _():
-            copy_to(goal, tx).start()
-
-    def bulk(k, rows):
-        def copy_to(goal, column):
+            for k in rows:
+                copy_of(k, along_x[m]).start()
+        for k in rows:
+            @pl.when(k > 0)
+            def _():
+                copy_of(k, tx).start()
+
+    def bulk(count):
+        def copy_of(k, column):
             return pltpu.make_async_remote_copy(
-                src_ref=message.at[16 * k + column, pl.ds(0, rows)], dst_ref=arrived.at[me, pl.ds(0, rows)],
-                send_sem=send_sems.at[rows - EARLY], recv_sem=recv_sem.at[k], device_id=(goal, column),
+                src_ref=message.at[16 * k + column, pl.ds(0, count)], dst_ref=arrived.at[me, pl.ds(0, count)],
+                send_sem=send_sems.at[count - EARLY], recv_sem=recv_sem.at[k], device_id=(goal_of(k), column),
                 device_id_type=MESH)
 
-        return copy_to
-
-    def deliver(k, carry):
-        chosen[k] = fill(k)
-        send_row(k, bulk(k, EARLY))
+        return copy_of
+
+    def deliver(pair, carry):
+        rows = (2 * pair, 2 * pair + 1)
+        for k in rows:
+            chosen[k] = fill(k)
+        send_rows(rows, bulk(EARLY))
         return carry
 
     pl.semaphore_wait(column_in, 15)
-    lax.fori_loop(0, SPLIT, deliver, 0)
+    lax.fori_loop(0, SPLIT // 2, deliver, 0)
     own_copy = pltpu.make_async_copy(message.at[tx, pl.ds(0, EARLY)], arrived.at[me, pl.ds(0, EARLY)], own_sems.at[0])
     own_copy.start()
 
@@ -354,29 +371,32 @@
     split_late[0:16, :] = high
     split_late[16:32, :] = rest
 
-    def deliver_late(k, carry):
-        parts = newest(chosen[k])
-        for h in range(2):
-            late[pl.ds(16 * k + 8 * h, 8), 0, :] = parts[h]
-
-        def copy_to(goal, column):
-            return pltpu.make_async_remote_copy(
-                src_ref=late.at[16 * k + column], dst_ref=late_in.at[me], send_sem=late_sems.at[0],
-                recv_sem=late_sems.at[1], device_id=(goal, column), device_id_type=MESH)
-
-        send_row(k, copy_to)
+    def late_copy(k, column):
+        return pltpu.make_async_remote_copy(
+            src_ref=late.at[16 * k + column], dst_ref=late_in.at[me], send_sem=late_sems.at[0],
+            recv_sem=late_sems.at[1], device_id=(goal_of(k), column), device_id_type=MESH)
+
+    def deliver_late(pair, carry):
+        rows = (2 * pair, 2 * pair + 1)
+        for k in rows:
+            parts = newest(chosen[k])
+            for h in range(2):
+                late[pl.ds(16 * k + 8 * h, 8), 0, :] = parts[h]
+        send_rows(rows, late_copy)
         return carry
 
-    lax.fori_loop(0, SPLIT, deliver_late, 0)
-
-    def deliver_all(k, carry):
-        parts = newest(fill(k))
-        for h in range(2):
-            message[pl.ds(16 * k + 8 * h, 8), EARLY, :] = parts[h]
-        send_row(k, bulk(k, EARLY + 1))
+    lax.fori_loop(0, SPLIT // 2, deliver_late, 0)
+
+    def deliver_all(pair, carry):
+        rows = (2 * pair, 2 * pair + 1)
+        for k in rows:
+            parts = newest(fill(k))
+            for h in range(2):
+                message[pl.ds(16 * k + 8 * h, 8), EARLY, :] = parts[h]
+        send_rows(rows, bulk(EARLY + 1))
         return carry
 
-    lax.fori_loop(SPLIT, 8, deliver_all, 0)
+    lax.fori_loop(SPLIT // 2, 4, deliver_all, 0)
     own_late = pltpu.make_async_copy(late.at[tx], late_in.at[me], own_sems.at[1])
     own_late.start()
 
@@ -391,7 +411,7 @@
             late_ref[kind, sender, 2 * h : 2 * h + 2, :] = part[2 * kind : 2 * kind + 2]
 
     def place_row(k, carry):
-        sender = lax.rem(ty - STRIDE * k + 64, 8)
+        sender = lax.rem(ty - offset(k) + 8, 8)
 
         @pl.when(k == 0)
         def _():
@@ -424,7 +444,7 @@
     sent = late.at[pl.ds(0, few)]
     pltpu.make_async_copy(sent, sent, late_sems.at[1]).wait()
     for k in range(SPLIT):
-        sender = lax.rem(ty - STRIDE * k + 64, 8)
+        sender = lax.rem(ty - offset(k) + 8, 8)
         for h in range(2):
             keep_late(sender, h, late_in[pl.ds(sender * 16 + 8 * h, 8), 0, :])
     for copy in edge_copies + packed_copies + spot_copies:
@@ -476,8 +496,9 @@
             pltpu.VMEM((8, 128), f32),
             pltpu.VMEM((8, 8, 128), f32),
             pltpu.VMEM((8, 8, 512), f32),
-            pltpu.VMEM((SPLIT, 256, 512), bf16),
-            pltpu.VMEM((256, 512), bf16),
+            pltpu.VMEM((SPLIT, 512, 256), bf16),
+            pltpu.VMEM((512, 128), i32),
+            pltpu.VMEM((512, 256), bf16),
             pltpu.VMEM((32, 512), bf16),
             pltpu.VMEM((32, 512), bf16),
             pltpu.VMEM((128, 24, 128), f32),

time: 37.2 us -> 36.9 us (level)
  no operation moved by 1% of the time
where the time goes in v4:
time: 36.9 us; the launch traced here: 36.6 us
  Pallas kernels  36.6 us (99%)
    pallas_call x1, Pallas kernels, per_device(): pl.pallas_call(advance_kernel, out_shape=(pltpu.VMEM((8, 288, 128), f32),...  34.5 us
    pallas_call x1, Pallas kernels, per_device(): pl.pallas_call(finish_kernel, out_shape=jax.ShapeDtypeStruct((SAMPLES, 32...  2.11 us

profile of v4, /device:TPU:1, one launch (start us, length us, event | category | flops | bytes accessed | tf_op | source)
XLA Modules:
  0.0 36.6 jit_solution(3926400358627033185)
XLA Ops:
  0.0 34.5 %advance.1 = (f32[8,288,128]{2,1,0:T(8,128)S(1)}, f32[3,8,4,128]{3,2,1,0:T(4,128)S(1)}, f32[2,512]{1,0:T(2,128)}) custom-call(s32[1,8]{1,0:T(1,128)} %leavers_ref.1, f32[2,3,128,128]{3,2,1,0:T(8,128)} %velocity_hbm.1, f32[2,512]{1,0:T(2,128)} %start_ref.1, s32[8,2,512]{2,1,0:T(2,128)} %bitcast.13, f32[568,128]{1,0:T(8,128)} %bitcast.12, s32[1,512]{1,0:T(1,128)} %bitcast.14, ...), custom_call_target="tpu_custom_call" | custom-call | tf_op jit(solution)/shard_map/advance/pallas_call | solution.py:479
  34.5 2.1 %finish.1 = f32[73,32,128]{2,1,0:T(8,128)} custom-call(f32[8,288,128]{2,1,0:T(8,128)S(1)} %get-tuple-element.7.slabs_ref, f32[3,8,4,128]{3,2,1,0:T(4,128)S(1)} %get-tuple-element.8.late_ref, f32[73,73]{1,0:T(8,128)} %filter_ref.3), custom_call_target="tpu_custom_call" | custom-call | tf_op jit(solution)/shard_map/finish/pallas_call | solution.py:525
